TPU v7x, 32 devices: a whole 2x2x4 slice. The times are simulated.
32 devices in a mesh: grp: 2 (over core), tp: 4 (over y, x), src: 4 (over z).
Axes of the slice: x: 2, y: 2, z: 4, core: 2. Of those that a mesh axis runs over, the one named last changes fastest.
Arguments:
- hidden_in: bfloat16 [512, 5120], P(('grp', 'src')), may hold values from -6 to 6
- attn_gain: float32 [5120], replicated, may hold values from 0.5 to 1.5
- w_qkv: int32 [1280, 5120], P(None, 'tp'), may hold values from -2147483648 to 2147483646
- qkv_scale: float32 [5120], P('tp'), may hold values from 0.0001118034 to 0.00041926274
- q_gain: float32 [128], replicated, may hold values from 0.25 to 1.75
- k_gain: float32 [128], replicated, may hold values from 0.1 to 1.9
- key_cache: bfloat16 [8, 64, 128, 512], P(('grp', 'src'), 'tp'), may hold values from -400 to 400
- value_cache: bfloat16 [8, 64, 128, 512], P(('grp', 'src'), 'tp'), may hold values from -9 to 9
- lengths: int32 [8, 64], P(('grp', 'src'), 'tp'), may hold values from 1 to 128, as said below
- w_out: int32 [1024, 5120], P('tp'), may hold values from -2147483648 to 2147483646
- out_scale: float32 [5120], replicated, may hold values from 0.0003125 to 0.00125
- mlp_gain: float32 [5120], replicated, may hold values from 0.5 to 1.5
- w_gate: int32 [1280, 12800], P(('grp', 'src'), 'tp'), may hold values from -2147483648 to 2147483646
- w_up: int32 [1280, 12800], P(('grp', 'src'), 'tp'), may hold values from -2147483648 to 2147483646
- gate_scale: float32 [12800], P('tp'), may hold values from 0.0001118034 to 0.00041926274
- up_scale: float32 [12800], P('tp'), may hold values from 0.0001118034 to 0.00041926274
- w_down: int32 [3200, 5120], P('tp', ('grp', 'src')), may hold values from -2147483648 to 2147483646
- down_scale: float32 [5120], replicated, may hold values from 0.00013258251 to 0.00053033006
Outputs:
- layer_out: bfloat16 [512, 5120], P(('grp', 'src'), 'tp')
Inputs may be any that keep to these rules, and one draw needn't show every extreme that they name: `lengths`: some sequence has exactly 128 cached positions.
All inputs are finite; a program needn't handle non-finite values.
Results may differ from a plain program's by a relative error of at most 0.028.
Values may be sent and summed in bfloat16 or wider, within the bound.
A program may use at most 128 MiB of HBM per device.

v0:
```python
import functools
import math

import jax
import jax.numpy as jnp
from jax import lax
from jax.experimental import pallas as pl
from jax.experimental.pallas import tpu as pltpu
from jax.sharding import PartitionSpec as P

D = 5120
QUERY_HEADS = 32
KEY_VALUE_HEADS = 4
HEAD_SIZE = 128
QUERY_COLUMNS = 4096
KEY_COLUMNS = 512


norm_epsilon = 1e-06
rope_base = 1000000.0


def unpack_bytes(packed, byte_index):
    return jnp.right_shift(jnp.left_shift(packed, 24 - 8 * byte_index), 24)


def byte_order(block):
    source = lax.broadcasted_iota(jnp.int32, (block, block), 0)
    target = lax.broadcasted_iota(jnp.int32, (block, block), 1)
    return (target == (source % 4) * (block // 4) + source // 4).astype(jnp.bfloat16)


def split_kernel(block, x_ref, order_ref, out_ref):
    lanes = block // 4
    for c in range(x_ref.shape[1] // block):
        moved = jnp.dot(
            x_ref[:, c * block : (c + 1) * block],
            order_ref[...],
            preferred_element_type=jnp.float32,
        ).astype(jnp.bfloat16)
        for j in range(4):
            out_ref[j, :, c * lanes : (c + 1) * lanes] = moved[:, j * lanes : (j + 1) * lanes]


def split_bytes(activations):
    rows, width = activations.shape
    if width % 512:
        return [activations[:, byte_index::4] for byte_index in range(4)]
    split = pl.pallas_call(
        functools.partial(split_kernel, 512),
        out_shape=jax.ShapeDtypeStruct((4, rows, width // 4), jnp.bfloat16),
        cost_estimate=pl.CostEstimate(
            flops=2 * rows * width * 512, bytes_accessed=4 * rows * width, transcendentals=0
        ),
        name="split_bytes",
    )(activations, byte_order(512))
    return [split[byte_index] for byte_index in range(4)]


def byte_product(activations, packed):
    pieces = split_bytes(activations)
    products = [
        jnp.dot(
            pieces[byte_index],
            unpack_bytes(packed, byte_index).astype(jnp.bfloat16),
            preferred_element_type=jnp.float32,
        )
        for byte_index in range(4)
    ]
    return products[0] + products[1] + products[2] + products[3]


def block_of(width):
    return math.gcd(640, width)


def order_kernel(block, x_ref, order_ref, out_ref):
    for c in range(x_ref.shape[1] // block):
        out_ref[:, c * block : (c + 1) * block] = jnp.dot(
            x_ref[:, c * block : (c + 1) * block],
            order_ref[...],
            preferred_element_type=jnp.float32,
        ).astype(jnp.bfloat16)


def order_bytes(activations):
    rows, width = activations.shape
    block = block_of(width)
    if block == width:
        return jnp.dot(activations, byte_order(block), preferred_element_type=jnp.float32).astype(
            jnp.bfloat16
        )
    return pl.pallas_call(
        functools.partial(order_kernel, block),
        out_shape=jax.ShapeDtypeStruct((rows, width), jnp.bfloat16),
        cost_estimate=pl.CostEstimate(
            flops=2 * rows * width * block, bytes_accessed=4 * rows * width, transcendentals=0
        ),
        name="order_bytes",
    )(activations, byte_order(block))


def unpack_ordered(packed):
    rows, columns = packed.shape
    block = block_of(4 * rows) // 4
    blocks = packed.reshape(rows // block, block, columns)
    parts = [unpack_bytes(blocks, j).astype(jnp.bfloat16) for j in range(4)]
    return jnp.stack(parts, axis=1).reshape(4 * rows, columns)


def normalize_rows(values, gain_row):
    return (
        values
        * lax.rsqrt(jnp.mean(values * values, axis=-1, keepdims=True) + norm_epsilon)
        * gain_row
    )


def rotary_embed(values, positions):
    half_dim = values.shape[-1] // 2
    freq_index = jnp.arange(half_dim, dtype=jnp.float32)
    inverse = jnp.exp(freq_index * (-math.log(rope_base) / half_dim))
    angles = positions.astype(jnp.float32)[:, None] * inverse[None, :]
    cosine = jnp.cos(angles)[:, None, :]
    sine_part = jnp.sin(angles)[:, None, :]
    lower_half = values[..., :half_dim]
    upper_half = values[..., half_dim:]
    return jnp.concatenate(
        [
            lower_half * cosine - upper_half * sine_part,
            upper_half * cosine + lower_half * sine_part,
        ],
        axis=-1,
    )


def local_attention(query_key_value_rows, q_gain, k_gain, stored_keys, stored_values, seq_lengths):
    count_of_rows = query_key_value_rows.shape[0]
    cache_length = stored_keys.shape[1]
    query_matrix = (
        query_key_value_rows[:, :QUERY_COLUMNS]
        .astype(jnp.float32)
        .reshape(count_of_rows, QUERY_HEADS, HEAD_SIZE)
    )
    incoming_keys = (
        query_key_value_rows[:, QUERY_COLUMNS : QUERY_COLUMNS + KEY_COLUMNS]
        .astype(jnp.float32)
        .reshape(count_of_rows, KEY_VALUE_HEADS, HEAD_SIZE)
    )
    incoming_values = query_key_value_rows[:, QUERY_COLUMNS + KEY_COLUMNS :].reshape(
        count_of_rows, KEY_VALUE_HEADS, HEAD_SIZE
    )
    query_matrix = rotary_embed(normalize_rows(query_matrix, q_gain), seq_lengths).astype(
        jnp.bfloat16
    )
    incoming_keys = rotary_embed(normalize_rows(incoming_keys, k_gain), seq_lengths).astype(
        jnp.bfloat16
    )
    query_groups = query_matrix.reshape(
        count_of_rows, KEY_VALUE_HEADS, QUERY_HEADS // KEY_VALUE_HEADS, HEAD_SIZE
    )
    key_slices = stored_keys.reshape(count_of_rows, cache_length, KEY_VALUE_HEADS, HEAD_SIZE)
    value_slices = stored_values.reshape(count_of_rows, cache_length, KEY_VALUE_HEADS, HEAD_SIZE)
    logit_scale = 1.0 / math.sqrt(HEAD_SIZE)
    scores = (
        jnp.einsum("bkgd,bpkd->bkgp", query_groups, key_slices, preferred_element_type=jnp.float32)
        * logit_scale
    )
    live_mask = jnp.arange(cache_length, dtype=jnp.int32)[None, :] < seq_lengths[:, None]
    scores = jnp.where(live_mask[:, None, None, :], scores, -jnp.inf)
    self_score = (
        jnp.einsum("nufi,nui->nuf", query_groups, incoming_keys, preferred_element_type=jnp.float32)
        * logit_scale
    )
    row_max = jnp.maximum(jnp.max(scores, axis=-1), self_score)
    soft_weights = jnp.exp(scores - row_max[..., None])
    own_weight = jnp.exp(self_score - row_max)
    denominator = jnp.sum(soft_weights, axis=-1) + own_weight
    own_low = lax.optimization_barrier(own_weight.astype(jnp.bfloat16)).astype(jnp.float32)
    numerator = jnp.einsum(
        "bkgp,bpkd->bkgd",
        soft_weights.astype(jnp.bfloat16),
        value_slices,
        preferred_element_type=jnp.float32,
    )
    numerator = numerator + own_low[..., None] * incoming_values.astype(jnp.float32)[:, :, None, :]
    return (
        (numerator / denominator[..., None])
        .reshape(count_of_rows, QUERY_COLUMNS)
        .astype(jnp.bfloat16)
    )


def summed_share(terms, tp_count):
    rows, columns = terms.shape
    pieces = lax.all_to_all(terms, "tp", split_axis=1, concat_axis=0, tiled=True)
    return jnp.sum(
        pieces.reshape(tp_count, rows, columns // tp_count).astype(jnp.float32), axis=0
    )


def gathered_rows(rows, axis):
    count = lax.axis_size(axis)
    copies = jnp.broadcast_to(rows[None], (count, *rows.shape))
    pieces = lax.all_to_all(copies, axis, split_axis=0, concat_axis=0)
    return pieces.reshape(count * rows.shape[0], rows.shape[1])


def summed_rows(terms, axis):
    count = lax.axis_size(axis)
    rows, columns = terms.shape
    pieces = lax.all_to_all(
        terms.reshape(count, rows // count, columns), axis, split_axis=0, concat_axis=0
    )
    return jnp.sum(pieces.astype(jnp.float32), axis=0)


def local(
    hidden_in,
    attn_gain,
    w_qkv,
    qkv_scale,
    q_gain,
    k_gain,
    key_cache,
    value_cache,
    lengths,
    w_out,
    out_scale,
    mlp_gain,
    w_gate,
    w_up,
    gate_scale,
    up_scale,
    w_down,
    down_scale,
):
    tp_count = lax.axis_size("tp")
    tp_index = lax.axis_index("tp")
    share_cols = D // tp_count
    residual = hidden_in.astype(jnp.float32)
    normed = normalize_rows(residual, attn_gain).astype(jnp.bfloat16)
    qkv_part = (byte_product(normed, w_qkv) * qkv_scale).astype(jnp.bfloat16)
    query_key_value_rows = lax.all_to_all(qkv_part, "tp", split_axis=0, concat_axis=1, tiled=True)
    heads_out = local_attention(
        query_key_value_rows, q_gain, k_gain, key_cache[0], value_cache[0], lengths[0]
    )
    head_rows = lax.all_to_all(heads_out, "tp", split_axis=1, concat_axis=0, tiled=True)
    partial_value = (byte_product(head_rows, w_out) * out_scale).astype(jnp.bfloat16)
    residual_share = lax.dynamic_slice_in_dim(hidden_in, tp_index * share_cols, share_cols, 1)
    mid_share = (
        residual_share.astype(jnp.float32) + summed_share(partial_value, tp_count)
    ).astype(jnp.bfloat16)
    mid_full = lax.all_gather(mid_share, "tp", axis=1, tiled=True)
    normed_mlp = normalize_rows(mid_full.astype(jnp.float32), mlp_gain).astype(jnp.bfloat16)
    mlp_columns = order_bytes(
        lax.all_to_all(normed_mlp, ("grp", "src"), split_axis=1, concat_axis=0, tiled=True)
    )
    gate_terms = jnp.dot(mlp_columns, unpack_ordered(w_gate), preferred_element_type=jnp.float32)
    up_terms = jnp.dot(mlp_columns, unpack_ordered(w_up), preferred_element_type=jnp.float32)
    both_terms = jnp.concatenate(
        [gate_terms.astype(jnp.bfloat16), up_terms.astype(jnp.bfloat16)], axis=1
    )
    both = summed_rows(summed_rows(both_terms, "grp").astype(jnp.bfloat16), "src")
    hidden = gate_scale.shape[0]
    gate_value = both[:, :hidden] * gate_scale
    up_value = both[:, hidden:] * up_scale
    activated = order_bytes((jax.nn.silu(gate_value) * up_value).astype(jnp.bfloat16))
    all_activated = gathered_rows(gathered_rows(activated, "src"), "grp")
    down_columns = jnp.dot(
        all_activated, unpack_ordered(w_down), preferred_element_type=jnp.float32
    ).astype(jnp.bfloat16)
    down_rows = lax.all_to_all(
        down_columns, ("grp", "src"), split_axis=0, concat_axis=1, tiled=True
    )
    down_share = lax.dynamic_slice_in_dim(down_scale, tp_index * share_cols, share_cols, 0)
    mlp_share = summed_share(down_rows, tp_count) * down_share
    return (mid_share.astype(jnp.float32) + mlp_share).astype(jnp.bfloat16)


def solution(mesh):
    return jax.shard_map(
        local,
        mesh=mesh,
        in_specs=(
            P(("grp", "src"), None),
            P(),
            P(None, "tp"),
            P("tp"),
            P(),
            P(),
            P(("grp", "src"), "tp", None, None),
            P(("grp", "src"), "tp", None, None),
            P(("grp", "src"), "tp"),
            P("tp", None),
            P(),
            P(),
            P(("grp", "src"), "tp"),
            P(("grp", "src"), "tp"),
            P("tp"),
            P("tp"),
            P("tp", ("grp", "src")),
            P(),
        ),
        out_specs=P(("grp", "src"), "tp"),
        check_vma=False,
    )
```

profile of v0, /device:TPU:0, one launch (start us, length us, event | category | flops | bytes accessed | tf_op | source)
XLA Modules:
  0.0 307.0 jit_solution(5775638950331051432)
XLA Ops:
  4.8 3.1 %split_bytes.2 = bf16[4,64,1280]{2,1,0:T(8,128)(2,1)} custom-call(bf16[64,5120]{1,0:T(8,128)(2,1)} %fusion.32.x_ref, bf16[512,512]{1,0:T(8,128)(2,1)} %fusion.51.order_ref), custom_call_target="tpu_custom_call" | custom-call | flops 335544320 | bytes 1310720 | tf_op jit(solution)/shard_map/split_bytes/pallas_call | solution.py:49
  7.9 4.1 %fusion.2 = f32[64,1280]{1,0:T(8,128)S(1)} fusion(s32[1280,1280]{1,0:T(8,128)} %param.20, bf16[4,64,1280]{2,1,0:T(8,128)(2,1)} %split_bytes.2), kind=kOutput, calls=%fused_computation.20 | convolution fusion | flops 214630400 | bytes 7045120 | tf_op jit(solution)/shard_map/dot_general | solution.py:63
  17.3 5.2 %all-to-all-start = ((bf16[4,16,1280]{2,1,0:T(8,128)(2,1)}), bf16[4,16,1280]{2,1,0:T(8,128)(2,1)S(1)}, u32[]{:S(2)}, u32[]{:S(2)}) async-start(bf16[4,16,1280]{2,1,0:T(8,128)(2,1)} %bitcast.5), calls=%async_computation | async-start | bytes 327680 | tf_op jit(solution)/shard_map/all_to_all | solution.py:244
  22.6 2.6 reshape_squeeze.6
  25.2 4.0 %reshape_squeeze.7 = bf16[16,128,4,128]{3,2,1,0:T(4,128)(2,1)} reshape(bf16[1,16,128,512]{3,2,1,0:T(8,128)(2,1)} %param.25) | data formatting | bytes 4194304 | tf_op jit(solution)/shard_map/reshape;squeeze | solution.py:163
  35.4 4.2 %all-to-all-start.1 = ((bf16[16,4,1024]{2,0,1:T(8,128)(2,1)}), bf16[16,4,1024]{2,0,1:T(8,128)(2,1)S(1)}, u32[]{:S(2)}, u32[]{:S(2)}) async-start(bf16[16,4,1024]{2,0,1:T(8,128)(2,1)} %copy.44), calls=%async_computation.1 | async-start | bytes 262144 | tf_op jit(solution)/shard_map/all_to_all | solution.py:248
  39.6 3.4 %fusion.52 = (bf16[1,1,160,3200]{3,2,1,0:T(8,128)(2,1)S(1)}, bf16[1,1,160,3200]{3,2,1,0:T(8,128)(2,1)S(1)}, bf16[1,1,160,3200]{3,2,1,0:T(8,128)(2,1)S(1)}, bf16[1,1,160,3200]{3,2,1,0:T(8,128)(2,1)}) fusion(s32[160,3200]{1,0:T(8,128)} %param.30), kind=kLoop, calls=%fused_computation.82 | loop fusion | flops 6144000 | bytes 6144000 | tf_op jit(solution)/shard_map/stack | solution.py:108
  47.3 3.5 %fusion.13 = f32[64,5120]{1,0:T(8,128)S(1)} fusion(s32[256,5120]{1,0:T(8,128)} %param.27, bf16[4,64,256]{2,1,0:T(8,128)(2,1)} %split_bytes.3), kind=kOutput, calls=%fused_computation.31 | convolution fusion | flops 171704320 | bytes 6586368 | tf_op jit(solution)/shard_map/dot_general | solution.py:63
  50.8 3.5 %convolution_add_fusion.2 = f32[64,5120]{1,0:T(8,128)S(1)} fusion(f32[64,5120]{1,0:T(8,128)S(1)} %fusion.13, s32[256,5120]{1,0:T(8,128)} %param.27, bf16[4,64,256]{2,1,0:T(8,128)(2,1)S(1)} %copy-done.9), kind=kOutput, calls=%fused_computation.10 | convolution fusion | flops 172032000 | bytes 7897088 | tf_op jit(solution)/shard_map/dot_general | solution.py:63
  56.9 4.3 %all-to-all-start.2 = ((bf16[64,4,1280]{2,0,1:T(8,128)(2,1)}), bf16[64,4,1280]{2,0,1:T(8,128)(2,1)}, u32[]{:S(2)}, u32[]{:S(2)}) async-start(bf16[64,4,1280]{2,0,1:T(8,128)(2,1)} %bitcast.112), calls=%async_computation.2 | async-start | bytes 1310720 | tf_op jit(solution)/shard_map/all_to_all | solution.py:196
  61.2 4.1 %fusion.56 = (bf16[1,1,160,3200]{3,2,1,0:T(8,128)(2,1)}, bf16[1,1,160,3200]{3,2,1,0:T(8,128)(2,1)}, bf16[1,1,160,3200]{3,2,1,0:T(8,128)(2,1)}, bf16[1,1,160,3200]{3,2,1,0:T(8,128)(2,1)}) fusion(s32[160,3200]{1,0:T(8,128)} %param.31), kind=kLoop, calls=%fused_computation.86 | loop fusion | flops 6144000 | bytes 6144000 | tf_op jit(solution)/shard_map/stack | solution.py:108
  65.4 3.5 %all-to-all-done.2 = bf16[64,4,1280]{2,0,1:T(8,128)(2,1)} async-done(((bf16[64,4,1280]{2,0,1:T(8,128)(2,1)}), bf16[64,4,1280]{2,0,1:T(8,128)(2,1)}, u32[]{:S(2)}, u32[]{:S(2)}) %all-to-all-start.2) | async-done | bytes 655392 | tf_op jit(solution)/shard_map/all_to_all | solution.py:196
  71.0 11.1 %all_gather.3 = bf16[64,5120]{1,0:T(8,128)(2,1)S(1)} all-gather(bf16[64,1280]{1,0:T(8,128)(2,1)S(1)} %add_convert_fusion.1), channel_id=1, replica_groups=mesh['grp'=2,'tp'=4,'src'=4] {'tp'}, dimensions={1}, use_global_device_ids=true | all-gather | bytes 819200 | tf_op jit(solution)/shard_map/all_gather | solution.py:254
  83.5 4.9 %all-to-all-start.3 = ((bf16[64,8,640]{2,0,1:T(8,128)(2,1)}), bf16[64,8,640]{2,0,1:T(8,128)(2,1)}, u32[]{:S(2)}, u32[]{:S(2)}) async-start(bf16[64,8,640]{2,0,1:T(8,128)(2,1)} %bitcast.113), calls=%async_computation.3 | async-start | bytes 1310720 | tf_op jit(solution)/shard_map/all_to_all | solution.py:257
  88.4 3.4 %pad_maximum_fusion.1 = bf16[1,4,160,3200]{3,2,1,0:T(8,128)(2,1)} fusion(bf16[1,1,160,3200]{3,2,1,0:T(8,128)(2,1)S(1)} %get-tuple-element.11, bf16[1,1,160,3200]{3,2,1,0:T(8,128)(2,1)} %get-tuple-element.12, bf16[1,1,160,3200]{3,2,1,0:T(8,128)(2,1)S(1)} %get-tuple-element.10, bf16[1,1,160,3200]{3,2,1,0:T(8,128)(2,1)S(1)} %get-tuple-element.9), kind=kLoop, calls=%fused_computation.17 | loop fusion | flops 6144000 | bytes 8192000 | tf_op jit(solution)/shard_map/stack | solution.py:108
  94.1 11.9 %all-to-all-done.3 = bf16[64,8,640]{2,0,1:T(8,128)(2,1)} async-done(((bf16[64,8,640]{2,0,1:T(8,128)(2,1)}), bf16[64,8,640]{2,0,1:T(8,128)(2,1)}, u32[]{:S(2)}, u32[]{:S(2)}) %all-to-all-start.3) | async-done | bytes 655392 | tf_op jit(solution)/shard_map/all_to_all | solution.py:257
  106.1 2.4 convolution_convert_fusion.2
  108.5 3.0 convolution_convert_fusion.1
  111.5 4.2 %convolution_convert_fusion = bf16[512,3200]{1,0:T(8,128)(2,1)} fusion(bf16[512,640]{1,0:T(8,128)(2,1)S(1)} %convolution_convert_fusion.2, bf16[640,3200]{1,0:T(8,128)(2,1)S(1)} %bitcast.104), kind=kOutput, calls=%fused_computation.6 | convolution fusion | flops 2098790400 | bytes 8028160 | tf_op jit(solution)/shard_map/dot_general | solution.py:260
  118.1 10.2 %all_to_all.116 = bf16[2,256,6400]{2,1,0:T(8,128)(2,1)} all-to-all(bf16[2,256,6400]{2,1,0:T(8,128)(2,1)S(1)} %bitcast.100), channel_id=1, replica_groups=mesh['grp'=2,'tp'=4,'src'=4] {'grp'}, dimensions={0} | all-to-all | bytes 13107200 | tf_op jit(solution)/shard_map/all_to_all | solution.py:212
  128.2 6.6 %reduce_sum.90 = bf16[256,6400]{1,0:T(8,128)(2,1)} reduce(bf16[2,256,6400]{2,1,0:T(8,128)(2,1)} %all_to_all.116, bf16[]{:T(256)} %constant.119.clone.1), dimensions={0}, to_apply=%region_7.8 | reduce | flops 1638400 | bytes 9830402 | tf_op jit(solution)/shard_map/reduce_sum | solution.py:215
  134.9 3.7 %all-to-all-start.5 = ((bf16[4,64,6400]{2,1,0:T(8,128)(2,1)}), bf16[4,64,6400]{2,1,0:T(8,128)(2,1)S(1)}, u32[]{:S(2)}, u32[]{:S(2)}) async-start(bf16[4,64,6400]{2,1,0:T(8,128)(2,1)} %bitcast.101), calls=%async_computation.5 | async-start | bytes 6553600 | tf_op jit(solution)/shard_map/all_to_all | solution.py:212
  140.6 72.0 %all-to-all-done.5 = bf16[4,64,6400]{2,1,0:T(8,128)(2,1)S(1)} async-done(((bf16[4,64,6400]{2,1,0:T(8,128)(2,1)}), bf16[4,64,6400]{2,1,0:T(8,128)(2,1)S(1)}, u32[]{:S(2)}, u32[]{:S(2)}) %all-to-all-start.5) | async-done | bytes 3276832 | tf_op jit(solution)/shard_map/all_to_all | solution.py:212
  214.1 2.8 order_bytes.1
  219.3 3.8 %all-to-all-start.6 = ((bf16[4,64,3200]{2,1,0:T(8,128)(2,1)}), bf16[4,64,3200]{2,1,0:T(8,128)(2,1)S(1)}, u32[]{:S(2)}, u32[]{:S(2)}) async-start(bf16[4,64,3200]{2,1,0:T(8,128)(2,1)} %broadcast_in_dim.16), calls=%async_computation.6 | async-start | bytes 3276800 | tf_op jit(solution)/shard_map/all_to_all | solution.py:205
  223.1 2.6 shift-right-arithmetic_convert_fusion.29
  227.9 33.0 %all-to-all-done.6 = bf16[4,64,3200]{2,1,0:T(8,128)(2,1)S(1)} async-done(((bf16[4,64,3200]{2,1,0:T(8,128)(2,1)}), bf16[4,64,3200]{2,1,0:T(8,128)(2,1)S(1)}, u32[]{:S(2)}, u32[]{:S(2)}) %all-to-all-start.6) | async-done | bytes 1638432 | tf_op jit(solution)/shard_map/all_to_all | solution.py:205
  261.1 6.6 %all_to_all.117 = bf16[2,256,3200]{2,1,0:T(8,128)(2,1)S(1)} all-to-all(bf16[2,256,3200]{2,1,0:T(8,128)(2,1)S(1)} %broadcast_in_dim.18), channel_id=1, replica_groups=mesh['grp'=2,'tp'=4,'src'=4] {'grp'}, dimensions={0} | all-to-all | bytes 6553600 | tf_op jit(solution)/shard_map/all_to_all | solution.py:205
  267.8 2.8 convolution_convert_fusion.3
  270.5 20.5 %all_to_all.118 = bf16[8,64,640]{2,1,0:T(8,128)(2,1)S(1)} all-to-all(bf16[8,64,640]{2,1,0:T(8,128)(2,1)S(1)} %bitcast.119), channel_id=1, replica_groups=mesh['grp'=2,'tp'=4,'src'=4] {'grp','src'}, dimensions={0} | all-to-all | bytes 1310720 | tf_op jit(solution)/shard_map/all_to_all | solution.py:273
  292.8 3.5 %all-to-all-start.9 = ((bf16[64,4,1280]{2,0,1:T(8,128)(2,1)}), bf16[64,4,1280]{2,0,1:T(8,128)(2,1)S(1)}, u32[]{:S(2)}, u32[]{:S(2)}) async-start(bf16[64,4,1280]{2,0,1:T(8,128)(2,1)} %copy.48), calls=%async_computation.9 | async-start | bytes 1310720 | tf_op jit(solution)/shard_map/all_to_all | solution.py:196
  297.0 9.2 %all-to-all-done.9 = bf16[64,4,1280]{2,0,1:T(8,128)(2,1)S(1)} async-done(((bf16[64,4,1280]{2,0,1:T(8,128)(2,1)}), bf16[64,4,1280]{2,0,1:T(8,128)(2,1)S(1)}, u32[]{:S(2)}, u32[]{:S(2)}) %all-to-all-start.9) | async-done | bytes 655392 | tf_op jit(solution)/shard_map/all_to_all | solution.py:196
  (110 shorter events, 42.9 us)
Async XLA Ops:
  7.9 4.8 %copy-start = (s32[1280,1280]{1,0:T(8,128)S(1)}, s32[1280,1280]{1,0:T(8,128)}, u32[]{:S(2)}) copy-start(s32[1280,1280]{1,0:T(8,128)} %param.20) | copy-start | bytes 19660804
  12.7 2.0 copy-start.8
  14.8 1.0 copy-start.15
  15.8 6.7 %copy-start.18 = (s32[1,16]{1,0:T(1,128)S(1)}, s32[1,16]{1,0:T(1,128)}, u32[]{:S(2)}) copy-start(s32[1,16]{1,0:T(1,128)} %param.26) | copy-start | bytes 196
  17.3 12.0 %all-to-all-start = ((bf16[4,16,1280]{2,1,0:T(8,128)(2,1)}), bf16[4,16,1280]{2,1,0:T(8,128)(2,1)S(1)}, u32[]{:S(2)}, u32[]{:S(2)}) async-start(bf16[4,16,1280]{2,1,0:T(8,128)(2,1)} %bitcast.5), calls=%async_computation | async-start | bytes 327680 | tf_op jit(solution)/shard_map/all_to_all | solution.py:244
  25.1 4.6 %copy-start.16 = (f32[128]{0:T(128)S(1)}, f32[128]{0:T(128)}, u32[]{:S(2)}) copy-start(f32[128]{0:T(128)} %param.23) | copy-start | bytes 1540
  25.1 4.7 %copy-start.17 = (f32[128]{0:T(128)S(1)}, f32[128]{0:T(128)}, u32[]{:S(2)}) copy-start(f32[128]{0:T(128)} %param.22) | copy-start | bytes 1540
  35.4 9.2 %all-to-all-start.1 = ((bf16[16,4,1024]{2,0,1:T(8,128)(2,1)}), bf16[16,4,1024]{2,0,1:T(8,128)(2,1)S(1)}, u32[]{:S(2)}, u32[]{:S(2)}) async-start(bf16[16,4,1024]{2,0,1:T(8,128)(2,1)} %copy.44), calls=%async_computation.1 | async-start | bytes 262144 | tf_op jit(solution)/shard_map/all_to_all | solution.py:248
  44.6 0.7 copy-start.10
  47.3 3.5 %copy-start.9 = (bf16[4,64,256]{2,1,0:T(8,128)(2,1)S(1)}, bf16[4,64,256]{2,1,0:T(8,128)(2,1)}, u32[]{:S(2)}) copy-start(bf16[4,64,256]{2,1,0:T(8,128)(2,1)} %split_bytes.3) | copy-start | bytes 393220
  47.3 7.0 %slice-start = ((s8[5242880]{0:T(1024)(128)(4,1)}), s8[4194304]{0:T(1024)(128)(4,1)S(1)}, s32[]{:S(2)}) async-start(s8[5242880]{0:T(1024)(128)(4,1)} %bitcast.98), calls=%async_computation.10 | async-start | bytes 8388608
  50.8 3.5 %slice-start.1 = ((s8[5242880]{0:T(1024)(128)(4,1)}), s8[1048576]{0:T(1024)(128)(4,1)S(1)}, s32[]{:S(2)}) async-start(s8[5242880]{0:T(1024)(128)(4,1)} %bitcast.98), calls=%async_computation.11 | async-start | bytes 2097152
  54.3 0.9 copy-start.11
  56.9 12.0 %all-to-all-start.2 = ((bf16[64,4,1280]{2,0,1:T(8,128)(2,1)}), bf16[64,4,1280]{2,0,1:T(8,128)(2,1)}, u32[]{:S(2)}, u32[]{:S(2)}) async-start(bf16[64,4,1280]{2,0,1:T(8,128)(2,1)} %bitcast.112), calls=%async_computation.2 | async-start | bytes 1310720 | tf_op jit(solution)/shard_map/all_to_all | solution.py:196
  65.3 17.0 %copy-start.12 = (f32[5120]{0:T(1024)S(1)}, f32[5120]{0:T(1024)}, u32[]{:S(2)}) copy-start(f32[5120]{0:T(1024)} %param.29) | copy-start | bytes 61444
  83.5 22.6 %all-to-all-start.3 = ((bf16[64,8,640]{2,0,1:T(8,128)(2,1)}), bf16[64,8,640]{2,0,1:T(8,128)(2,1)}, u32[]{:S(2)}, u32[]{:S(2)}) async-start(bf16[64,8,640]{2,0,1:T(8,128)(2,1)} %bitcast.113), calls=%async_computation.3 | async-start | bytes 1310720 | tf_op jit(solution)/shard_map/all_to_all | solution.py:257
  88.4 3.5 %copy-start.4 = (bf16[1,1,160,3200]{3,2,1,0:T(8,128)(2,1)S(1)}, bf16[1,1,160,3200]{3,2,1,0:T(8,128)(2,1)}, u32[]{:S(2)}) copy-start(bf16[1,1,160,3200]{3,2,1,0:T(8,128)(2,1)} %get-tuple-element.13) | copy-start | bytes 3072004
  88.4 3.5 %copy-start.5 = (bf16[1,1,160,3200]{3,2,1,0:T(8,128)(2,1)S(1)}, bf16[1,1,160,3200]{3,2,1,0:T(8,128)(2,1)}, u32[]{:S(2)}) copy-start(bf16[1,1,160,3200]{3,2,1,0:T(8,128)(2,1)} %get-tuple-element.14) | copy-start | bytes 3072004
  88.4 3.4 %copy-start.6 = (bf16[1,1,160,3200]{3,2,1,0:T(8,128)(2,1)S(1)}, bf16[1,1,160,3200]{3,2,1,0:T(8,128)(2,1)}, u32[]{:S(2)}) copy-start(bf16[1,1,160,3200]{3,2,1,0:T(8,128)(2,1)} %get-tuple-element.15) | copy-start | bytes 3072004
  88.4 3.4 %copy-start.7 = (bf16[1,1,160,3200]{3,2,1,0:T(8,128)(2,1)S(1)}, bf16[1,1,160,3200]{3,2,1,0:T(8,128)(2,1)}, u32[]{:S(2)}) copy-start(bf16[1,1,160,3200]{3,2,1,0:T(8,128)(2,1)} %get-tuple-element.16) | copy-start | bytes 3072004
  106.1 2.4 copy-start.1
  108.5 3.0 copy-start.2
  134.9 77.7 %all-to-all-start.5 = ((bf16[4,64,6400]{2,1,0:T(8,128)(2,1)}), bf16[4,64,6400]{2,1,0:T(8,128)(2,1)S(1)}, u32[]{:S(2)}, u32[]{:S(2)}) async-start(bf16[4,64,6400]{2,1,0:T(8,128)(2,1)} %bitcast.101), calls=%async_computation.5 | async-start | bytes 6553600 | tf_op jit(solution)/shard_map/all_to_all | solution.py:212
  140.6 72.5 %copy-start.13 = (f32[3200]{0:T(1024)S(1)}, f32[3200]{0:T(1024)}, u32[]{:S(2)}) copy-start(f32[3200]{0:T(1024)} %param.33) | copy-start | bytes 38404
  140.6 72.5 %copy-start.14 = (f32[3200]{0:T(1024)S(1)}, f32[3200]{0:T(1024)}, u32[]{:S(2)}) copy-start(f32[3200]{0:T(1024)} %param.32) | copy-start | bytes 38404
  219.3 41.6 %all-to-all-start.6 = ((bf16[4,64,3200]{2,1,0:T(8,128)(2,1)}), bf16[4,64,3200]{2,1,0:T(8,128)(2,1)S(1)}, u32[]{:S(2)}, u32[]{:S(2)}) async-start(bf16[4,64,3200]{2,1,0:T(8,128)(2,1)} %broadcast_in_dim.16), calls=%async_computation.6 | async-start | bytes 3276800 | tf_op jit(solution)/shard_map/all_to_all | solution.py:205
  261.1 6.6 %copy-start.3 = (bf16[5,4,160,640]{3,2,1,0:T(8,128)(2,1)S(1)}, bf16[5,4,160,640]{3,2,1,0:T(8,128)(2,1)}, u32[]{:S(2)}) copy-start(bf16[5,4,160,640]{3,2,1,0:T(8,128)(2,1)} %pad_maximum_fusion.3) | copy-start | bytes 12288004
  292.8 13.4 %all-to-all-start.9 = ((bf16[64,4,1280]{2,0,1:T(8,128)(2,1)}), bf16[64,4,1280]{2,0,1:T(8,128)(2,1)S(1)}, u32[]{:S(2)}, u32[]{:S(2)}) async-start(bf16[64,4,1280]{2,0,1:T(8,128)(2,1)} %copy.48), calls=%async_computation.9 | async-start | bytes 1310720 | tf_op jit(solution)/shard_map/all_to_all | solution.py:196
where the time goes:
time: 308 us; the launch traced here: 307 us
  waiting for transfers between devices  131 us (43%)
  blocking collectives  48.4 us (16%)
  other arithmetic  40.1 us (13%)
  matrix products  33.5 us (11%)
  starting transfers between devices  29.6 us (10%)
  local copies, waits for them, and re-layouts  15.7 us (5%)
  Pallas kernels  7.98 us (3%)
    all_to_all x1, waiting for transfers between devices, summed_rows(): lax.all_to_all(terms.reshape(count, rows // count, columns), axis, split_...  72 us
    all_to_all x1, waiting for transfers between devices, gathered_rows(): pieces = lax.all_to_all(copies, axis, split_axis=0, concat_axis=0)  33 us
    all_to_all x1, blocking collectives, local(): lax.all_to_all(down_columns, ('grp', 'src'), split_axis=0, concat_axis=1,...  20.5 us
    dot_general x8, matrix products, byte_product(): jnp.dot(pieces[byte_index], unpack_bytes(packed, byte_index).astype(jnp.b...  17.2 us
    another operation x5, other arithmetic, unpack_ordered(): return jnp.stack(parts, axis=1).reshape(4 * rows, columns)  15.5 us
    all_to_all x2, waiting for transfers between devices, summed_share(): lax.all_to_all(terms, 'tp', split_axis=1, concat_axis=0, tiled=True)  12.6 us
    all_to_all x1, waiting for transfers between devices, local(): lax.all_to_all(normed_mlp, ('grp', 'src'), split_axis=1, concat_axis=0, t...  11.9 us
    all_gather x1, blocking collectives, local(): mid_full = lax.all_gather(mid_share, 'tp', axis=1, tiled=True)  11.1 us
  transfers between devices with their start and end apart: 7, of which 6 were waited for; matrix products, arithmetic and copies ran while one was open for 9% of the time, Pallas kernels for 0%

commit v1 on v0

--- a/solution.py
+++ b/solution.py
@@ -213,6 +213,382 @@
         terms.reshape(count, rows // count, columns), axis, split_axis=0, concat_axis=0
     )
     return jnp.sum(pieces.astype(jnp.float32), axis=0)
+
+
+LANES = 128
+MESH = pl.DeviceIdType.MESH
+
+
+def lane_order(block):
+    source = lax.broadcasted_iota(jnp.int32, (block, block), 0)
+    target = lax.broadcasted_iota(jnp.int32, (block, block), 1)
+    return (target == (source % 4) * (block // 4) + source // 4).astype(jnp.bfloat16)
+
+
+def unpack_slab(packed):
+    rows, columns = packed.shape
+    slab = LANES // 4
+    parts = []
+    for k in range(rows // slab):
+        words = packed[k * slab : (k + 1) * slab]
+        for j in range(4):
+            parts.append(unpack_bytes(words, j).astype(jnp.float32).astype(jnp.bfloat16))
+    return jnp.concatenate(parts, axis=0)
+
+
+def mlp_kernel(
+    lag,
+    x_ref,
+    gate_own,
+    gate_other,
+    up_own,
+    up_other,
+    down_own,
+    down_other,
+    gate_scale,
+    up_scale,
+    down_scale,
+    mid_ref,
+    order_ref,
+    out_ref,
+    gate_v,
+    up_v,
+    down_v,
+    x_v,
+    partial,
+    sum_send,
+    sum_recv,
+    act,
+    total,
+    part_send,
+    part_recv,
+    load_sem,
+    sum_send_sem,
+    sum_recv_sem,
+    act_send_sem,
+    act_recv_sem,
+    part_send_sem,
+    part_recv_sem,
+):
+    g, t, s = lax.axis_index("grp"), lax.axis_index("tp"), lax.axis_index("src")
+    count_g, count_t, count_s = lax.axis_size("grp"), lax.axis_size("tp"), lax.axis_size("src")
+    rows = x_ref.shape[0]
+    half = rows // 2
+    packed_rows, hidden = gate_own.shape
+    block = down_own.shape[1]
+    chunks = hidden // LANES
+    groups = load_sem.shape[1]
+    width = hidden // groups
+    per_group = chunks // groups
+    group_rows = rows // count_s
+
+    def load(array, index):
+        source = (gate_own, gate_other, up_own, up_other)[array]
+        target = (gate_v, gate_v, up_v, up_v)[array]
+        columns = pl.ds(pl.multiple_of(index * width, LANES), width)
+        return pltpu.make_async_copy(
+            source.at[:, columns], target.at[array % 2, :, columns], load_sem.at[array, index]
+        )
+
+    def load_down(index):
+        source = (down_own, down_other)[index]
+        return pltpu.make_async_copy(source, down_v.at[index], load_sem.at[4 + index, 0])
+
+    for index in range(groups):
+        for array in range(4):
+            load(array, index).start()
+    for index in range(2):
+        load_down(index).start()
+
+    barrier = pltpu.get_barrier_semaphore()
+    for tt in range(count_t):
+        for ss in range(count_s):
+
+            @pl.when((tt != t) | (ss != s))
+            def _():
+                pl.semaphore_signal(
+                    barrier, inc=1, device_id={"tp": tt, "src": ss}, device_id_type=MESH
+                )
+
+    total[...] = jnp.zeros_like(total)
+    blocks = x_ref.shape[1] // LANES
+    stacked = jnp.concatenate(
+        [x_ref[:, k * LANES : (k + 1) * LANES] for k in range(blocks)], axis=0
+    )
+    moved = jnp.dot(stacked, order_ref[...], preferred_element_type=jnp.float32).astype(
+        jnp.bfloat16
+    )
+    for k in range(blocks):
+        x_v[:, k * LANES : (k + 1) * LANES] = moved[k * rows : (k + 1) * rows]
+    pl.semaphore_wait(barrier, count_t * count_s - 1)
+
+    last = count_s - 1
+    far = last * lag
+    toward = (s - 1, s + 1)
+
+    def sum_copy(side, j):
+        return pltpu.make_async_remote_copy(
+            src_ref=sum_send.at[side, j],
+            dst_ref=sum_recv.at[side, j],
+            send_sem=sum_send_sem.at[side, j],
+            recv_sem=sum_recv_sem.at[side, j],
+            device_id={"src": toward[side]},
+            device_id_type=MESH,
+        )
+
+    def act_copy(side, j):
+        return pltpu.make_async_remote_copy(
+            src_ref=act.at[j, side],
+            dst_ref=act.at[j, side],
+            send_sem=act_send_sem.at[side, j],
+            recv_sem=act_recv_sem.at[side, j],
+            device_id={"src": toward[1 - side]},
+            device_id_type=MESH,
+        )
+
+    def depth_of(side):
+        return last - s if side == 0 else s
+
+    def sum_step(side, j):
+        depth = depth_of(side)
+        at_end = depth == last
+
+        @pl.when(depth > 0)
+        def _():
+            sum_copy(side, j).wait_recv()
+
+        @pl.when(depth == 0)
+        def _():
+            sum_send[side, j] = partial[j, side].astype(jnp.bfloat16)
+            sum_copy(side, j).start()
+
+        @pl.when((depth > 0) & jnp.logical_not(at_end))
+        def _():
+            sum_send[side, j] = (
+                partial[j, side] + sum_recv[side, j].astype(jnp.float32)
+            ).astype(jnp.bfloat16)
+            sum_copy(side, j).start()
+
+        @pl.when(at_end)
+        def _():
+            value = partial[j, side] + sum_recv[side, j].astype(jnp.float32)
+            columns = pl.ds(pl.multiple_of(j * LANES, LANES), LANES)
+            gate_value = value[:, :LANES] * gate_scale[:, columns]
+            up_value = value[:, LANES:] * up_scale[:, columns]
+            activated = (gate_value / (1.0 + jnp.exp(-gate_value)) * up_value).astype(jnp.bfloat16)
+            act[j, side] = jnp.dot(
+                activated, order_ref[...], preferred_element_type=jnp.float32
+            ).astype(jnp.bfloat16)
+            act_copy(side, j).start()
+
+    def act_step(side, j):
+        depth = last - depth_of(side)
+        act_copy(side, j).wait_recv()
+
+        @pl.when(depth < last)
+        def _():
+            act_copy(side, j).start()
+
+    def step(i, carry):
+        @pl.when(i < chunks)
+        def _():
+            @pl.when(lax.rem(i, per_group) == 0)
+            def _():
+                for array in range(4):
+                    load(array, i // per_group).wait()
+
+            columns = pl.ds(pl.multiple_of(i * LANES, LANES), LANES)
+            gate_w = [unpack_slab(gate_v[index, :, columns]) for index in range(2)]
+            up_w = [unpack_slab(up_v[index, :, columns]) for index in range(2)]
+            weights = jnp.concatenate(
+                [jnp.concatenate(gate_w, axis=0), jnp.concatenate(up_w, axis=0)], axis=1
+            )
+            product = jnp.dot(x_v[...], weights, preferred_element_type=jnp.float32)
+            partial[i, 0] = product[:half]
+            partial[i, 1] = product[half:]
+
+        for side in range(2):
+            j = i - depth_of(side) * lag
+
+            @pl.when((j >= 0) & (j < chunks))
+            def _():
+                sum_step(side, j)
+
+        for side in range(2):
+            depth = last - depth_of(side)
+            j = i - far - depth * lag
+
+            @pl.when((depth > 0) & (j >= 0) & (j < chunks))
+            def _():
+                act_step(side, j)
+
+        j = i - far - jnp.maximum(s, last - s) * lag
+
+        @pl.when((j >= 0) & (j < chunks))
+        def _():
+            @pl.when(j == 0)
+            def _():
+                for index in range(2):
+                    load_down(index).wait()
+
+            slab = LANES // 4
+            words = pl.ds(pl.multiple_of(j * slab, slab), slab)
+            weights = jnp.concatenate(
+                [unpack_slab(down_v[index, words, :]) for index in range(2)], axis=1
+            )
+            for side in range(2):
+                total[side * half : (side + 1) * half] += jnp.dot(
+                    act[j, side], weights, preferred_element_type=jnp.float32
+                )
+
+        return carry
+
+    lax.fori_loop(0, chunks + 2 * far, step, 0)
+
+    per_share = count_g * count_s // count_t
+
+    def part_copy(index, ss):
+        number = jnp.where(index == 0, g, count_g - 1 - g) * count_s + s
+        owner = number // per_share
+        slot = t * per_share + lax.rem(number, per_share)
+        return owner, slot, pltpu.make_async_remote_copy(
+            src_ref=part_send.at[index, ss],
+            dst_ref=part_recv.at[slot],
+            send_sem=part_send_sem.at[index, ss],
+            recv_sem=part_recv_sem.at[slot],
+            device_id={"tp": owner, "src": ss},
+            device_id_type=MESH,
+        )
+
+    for shift in range(count_s):
+        ss = lax.rem(s + 1 + shift, count_s)
+        row = pl.ds(pl.multiple_of(ss * group_rows, group_rows), group_rows)
+        for index in range(2):
+            owner, slot, copy = part_copy(index, ss)
+            piece = total[row, index * block : (index + 1) * block].astype(jnp.bfloat16)
+            mine = (owner == t) & (ss == s)
+
+            @pl.when(mine)
+            def _():
+                part_recv[slot] = piece
+
+            @pl.when(jnp.logical_not(mine))
+            def _():
+                part_send[index, ss] = piece
+                copy.start()
+
+    for slot in range(count_t * per_share):
+        number = t * per_share + slot % per_share
+        from_me = (slot // per_share == t) & (lax.rem(number, count_s) == s)
+
+        @pl.when(jnp.logical_not(from_me))
+        def _():
+            pltpu.make_async_remote_copy(
+                src_ref=part_send.at[0, 0],
+                dst_ref=part_recv.at[slot],
+                send_sem=part_send_sem.at[0, 0],
+                recv_sem=part_recv_sem.at[slot],
+                device_id={"tp": t, "src": s},
+                device_id_type=MESH,
+            ).wait_recv()
+
+    for place in range(per_share):
+        value = part_recv[place].astype(jnp.float32)
+        for tt in range(1, count_t):
+            value += part_recv[tt * per_share + place].astype(jnp.float32)
+        columns = slice(place * block, (place + 1) * block)
+        out_ref[:, columns] = (
+            mid_ref[:, columns].astype(jnp.float32) + value * down_scale[:, columns]
+        ).astype(jnp.bfloat16)
+
+    for ss in range(count_s):
+        for index in range(2):
+            owner, slot, copy = part_copy(index, ss)
+
+            @pl.when((owner != t) | (ss != s))
+            def _():
+                copy.wait_send()
+
+    def drain(j, carry):
+        for side in range(2):
+            depth = depth_of(side)
+
+            @pl.when(depth < last)
+            def _():
+                sum_copy(side, j).wait_send()
+
+            @pl.when(depth > 0)
+            def _():
+                act_copy(side, j).wait_send()
+
+        return carry
+
+    lax.fori_loop(0, chunks, drain, 0)
+
+
+def mlp_block(x, gate, up, down, gate_scale, up_scale, down_scale, mid, lag):
+    count_t, count_s = lax.axis_size("tp"), lax.axis_size("src")
+    rows, depth = x.shape
+    packed_rows, hidden = gate[0].shape
+    packed_hidden, block = down[0].shape
+    chunks = hidden // LANES
+    groups = 5 if chunks % 5 == 0 else 1
+    half = rows // 2
+    group_rows = rows // count_s
+    slots = count_t * (mid.shape[1] // block)
+    bf16, f32 = jnp.bfloat16, jnp.float32
+    vmem = pl.BlockSpec(memory_space=pltpu.VMEM)
+    hbm = pl.BlockSpec(memory_space=pl.ANY)
+    return pl.pallas_call(
+        functools.partial(mlp_kernel, lag),
+        out_shape=jax.ShapeDtypeStruct(mid.shape, bf16),
+        in_specs=[vmem] + [hbm] * 6 + [vmem] * 5,
+        out_specs=vmem,
+        scratch_shapes=[
+            pltpu.VMEM((2, packed_rows, hidden), jnp.int32),
+            pltpu.VMEM((2, packed_rows, hidden), jnp.int32),
+            pltpu.VMEM((2, packed_hidden, block), jnp.int32),
+            pltpu.VMEM((rows, depth), bf16),
+            pltpu.VMEM((chunks, 2, half, 2 * LANES), f32),
+            pltpu.VMEM((2, chunks, half, 2 * LANES), bf16),
+            pltpu.VMEM((2, chunks, half, 2 * LANES), bf16),
+            pltpu.VMEM((chunks, 2, half, LANES), bf16),
+            pltpu.VMEM((rows, depth), f32),
+            pltpu.VMEM((2, count_s, group_rows, block), bf16),
+            pltpu.VMEM((slots, group_rows, block), bf16),
+            pltpu.SemaphoreType.DMA((6, groups)),
+            pltpu.SemaphoreType.DMA((2, chunks)),
+            pltpu.SemaphoreType.DMA((2, chunks)),
+            pltpu.SemaphoreType.DMA((2, chunks)),
+            pltpu.SemaphoreType.DMA((2, chunks)),
+            pltpu.SemaphoreType.DMA((2, count_s)),
+            pltpu.SemaphoreType.DMA((slots,)),
+        ],
+        compiler_params=pltpu.CompilerParams(
+            collective_id=1, has_side_effects=True, vmem_limit_bytes=56 * 1024 * 1024
+        ),
+        cost_estimate=pl.CostEstimate(
+            flops=2 * rows * depth * hidden * 3,
+            bytes_accessed=4 * 3 * 2 * packed_rows * hidden,
+            transcendentals=rows * hidden,
+        ),
+        name="mlp_block",
+    )(x, *gate, *up, *down, gate_scale, up_scale, down_scale, mid, lane_order(LANES))
+
+
+def fast_mlp(grp, tp, src, args):
+    w_gate, w_down, hidden_in = args
+    rows = hidden_in.shape[0]
+    return (
+        grp == 2
+        and src > 1
+        and (grp * src) % tp == 0
+        and w_gate.shape[0] % 32 == 0
+        and w_gate.shape[1] % LANES == 0
+        and w_down.shape[1] % LANES == 0
+        and rows % 16 == 0
+        and (rows * src) % 32 == 0
+    )
 
 
 def local(
@@ -253,6 +629,34 @@
     ).astype(jnp.bfloat16)
     mid_full = lax.all_gather(mid_share, "tp", axis=1, tiled=True)
     normed_mlp = normalize_rows(mid_full.astype(jnp.float32), mlp_gain).astype(jnp.bfloat16)
+    if fast_mlp(lax.axis_size("grp"), tp_count, lax.axis_size("src"), (w_gate, w_down, hidden_in)):
+        g = lax.axis_index("grp")
+        count_s = lax.axis_size("src")
+        rows = hidden_in.shape[0]
+        swap = [(0, 1), (1, 0)]
+        gate = (w_gate, lax.ppermute(w_gate, "grp", swap))
+        up = (w_up, lax.ppermute(w_up, "grp", swap))
+        down = (w_down, lax.ppermute(w_down, "grp", swap))
+        width = D // 2
+        own = lax.dynamic_slice_in_dim(normed_mlp, g * width, width, 1)
+        other = lax.dynamic_slice_in_dim(normed_mlp, (1 - g) * width, width, 1)
+        both = jnp.concatenate(
+            [own.reshape(rows, count_s, -1), other.reshape(rows, count_s, -1)], axis=2
+        )
+        x = lax.all_to_all(both, "src", split_axis=1, concat_axis=0, tiled=True)
+        x = x.reshape(rows * count_s, -1)
+        down_share = lax.dynamic_slice_in_dim(down_scale, tp_index * share_cols, share_cols, 0)
+        return mlp_block(
+            x,
+            gate,
+            up,
+            down,
+            gate_scale[None],
+            up_scale[None],
+            down_share[None],
+            mid_share,
+            2,
+        )
     mlp_columns = order_bytes(
         lax.all_to_all(normed_mlp, ("grp", "src"), split_axis=1, concat_axis=0, tiled=True)
     )

time: 308 us -> 185 us (0.60)
  waiting for transfers between devices: 131 us -> 16.7 us
  Pallas kernels: 7.98 us -> 88.3 us
  other arithmetic: 40.1 us -> 8.75 us
  blocking collectives: 48.4 us -> 20.4 us
  starting transfers between devices: 29.6 us -> 14.2 us
  matrix products: 33.5 us -> 21.1 us
    all_to_all x4 -> x1, waiting for transfers between devices: 119 us -> 9.68 us  [local(): x = lax.all_to_all(both, 'src', split_axis=1, concat_axis=0, tiled=True)]
    pallas_call x1, Pallas kernels: 2.82 us -> 83.1 us  [mlp_block(): pl.pallas_call(functools.partial(mlp_kernel, lag), out_shape=jax.ShapeDty...]
    all_to_all x3 -> x1, blocking collectives: 37.3 us -> 9.11 us  [local(): lax.all_to_all(heads_out, 'tp', split_axis=1, concat_axis=0, tiled=True)]
    another operation x6 -> x1, other arithmetic: 15.6 us -> 0.09 us  [the longest x5 15.5 us: unpack_ordered(): return jnp.stack(parts, axis=1).reshape(4 * rows, columns)]
    dot_general x4 -> x0, matrix products: 12.4 us -> none  [the longest x1 4.18 us: local(): jnp.dot(mlp_columns, unpack_ordered(w_up), preferred_element_type=jnp.flo...]
    all_to_all x4 -> x1, starting transfers between devices: 16.6 us -> 4.87 us  [local(): x = lax.all_to_all(both, 'src', split_axis=1, concat_axis=0, tiled=True)]
    reduce_sum x2 -> x0, other arithmetic: 7.09 us -> none  [summed_rows(): return jnp.sum(pieces.astype(jnp.float32), axis=0)]
    all_to_all x2 -> x1, waiting for transfers between devices: 12.6 us -> 7.05 us  [summed_share(): lax.all_to_all(terms, 'tp', split_axis=1, concat_axis=0, tiled=True)]
  transfers between devices with their start and end apart: 7 -> 6, of which waited for: 6 -> 2; matrix products, arithmetic and copies ran while one was open for 9% -> 7% of each run, Pallas kernels for 0% -> 0%
where the time goes in v1:
time: 185 us; the launch traced here: 184 us
  Pallas kernels  88.3 us (48%)
  matrix products  21.1 us (11%)
  blocking collectives  20.4 us (11%)
  waiting for transfers between devices  16.7 us (9%)
  local copies, waits for them, and re-layouts  14.5 us (8%)
  starting transfers between devices  14.2 us (8%)
  other arithmetic  8.75 us (5%)
    pallas_call x1, Pallas kernels, mlp_block(): pl.pallas_call(functools.partial(mlp_kernel, lag), out_shape=jax.ShapeDty...  83.1 us
    dot_general x8, matrix products, byte_product(): jnp.dot(pieces[byte_index], unpack_bytes(packed, byte_index).astype(jnp.b...  17.2 us
    all_gather x1, blocking collectives, local(): mid_full = lax.all_gather(mid_share, 'tp', axis=1, tiled=True)  11.3 us
    all_to_all x1, waiting for transfers between devices, local(): x = lax.all_to_all(both, 'src', split_axis=1, concat_axis=0, tiled=True)  9.68 us
    all_to_all x1, blocking collectives, local(): lax.all_to_all(heads_out, 'tp', split_axis=1, concat_axis=0, tiled=True)  9.11 us
    all_to_all x1, waiting for transfers between devices, summed_share(): lax.all_to_all(terms, 'tp', split_axis=1, concat_axis=0, tiled=True)  7.05 us
    all_to_all x1, starting transfers between devices, local(): lax.all_to_all(qkv_part, 'tp', split_axis=0, concat_axis=1, tiled=True)  5.2 us
    pallas_call x2, Pallas kernels, split_bytes(): pl.pallas_call(functools.partial(split_kernel, 512), out_shape=jax.ShapeD...  5.17 us
  transfers between devices with their start and end apart: 6, of which 2 were waited for; matrix products, arithmetic and copies ran while one was open for 7% of the time, Pallas kernels for 0%

profile of v1, /device:TPU:0, one launch (start us, length us, event | category | flops | bytes accessed | tf_op | source)
XLA Modules:
  0.0 184.5 jit_solution(8496038873569473690)
XLA Ops:
  0.0 1.3 fusion.30
  1.3 2.2 %fusion.32.x_ref = bf16[64,5120]{1,0:T(8,128)(2,1)} fusion(bf16[64,5120]{1,0:T(8,128)(2,1)} %param.18, f32[5120]{0:T(1024)} %param.19, f32[64]{0:T(128)S(1)} %add_rsqrt_fusion.3), kind=kLoop, calls=%fused_computation.47 | loop fusion | flops 1310720 | bytes 1331456 | tf_op jit(solution)/shard_map/convert_element_type | solution.py:618
  3.5 1.3 fusion.51.order_ref
  4.8 3.1 %split_bytes.2 = bf16[4,64,1280]{2,1,0:T(8,128)(2,1)} custom-call(bf16[64,5120]{1,0:T(8,128)(2,1)} %fusion.32.x_ref, bf16[512,512]{1,0:T(8,128)(2,1)} %fusion.51.order_ref), custom_call_target="tpu_custom_call" | custom-call | flops 335544320 | bytes 1310720 | tf_op jit(solution)/shard_map/split_bytes/pallas_call | solution.py:49
  7.9 4.1 %fusion.2 = f32[64,1280]{1,0:T(8,128)S(1)} fusion(s32[1280,1280]{1,0:T(8,128)} %param.20, bf16[4,64,1280]{2,1,0:T(8,128)(2,1)} %split_bytes.2), kind=kOutput, calls=%fused_computation.13 | convolution fusion | flops 214630400 | bytes 7045120 | tf_op jit(solution)/shard_map/dot_general | solution.py:63
  12.7 2.0 %fusion.23 = f32[64,1280]{1,0:T(8,128)S(1)} fusion(f32[64,1280]{1,0:T(8,128)S(1)} %fusion.2, s32[1280,1280]{1,0:T(8,128)S(1)} %copy-done, bf16[4,64,1280]{2,1,0:T(8,128)(2,1)} %split_bytes.2), kind=kOutput, calls=%fused_computation.34 | convolution fusion | flops 214712320 | bytes 7372800 | tf_op jit(solution)/shard_map/dot_general | solution.py:63
  14.8 1.0 fusion.22
  15.8 1.5 fusion.25
  17.3 5.2 %all-to-all-start = ((bf16[4,16,1280]{2,1,0:T(8,128)(2,1)}), bf16[4,16,1280]{2,1,0:T(8,128)(2,1)S(1)}, u32[]{:S(2)}, u32[]{:S(2)}) async-start(bf16[4,16,1280]{2,1,0:T(8,128)(2,1)} %bitcast.5), calls=%async_computation | async-start | bytes 327680 | tf_op jit(solution)/shard_map/all_to_all | solution.py:620
  22.5 2.6 %reshape_squeeze.6 = bf16[16,128,4,128]{3,2,1,0:T(4,128)(2,1)S(1)} reshape(bf16[1,16,128,512]{3,2,1,0:T(8,128)(2,1)} %param.24) | data formatting | bytes 4194304 | tf_op jit(solution)/shard_map/reshape;squeeze | solution.py:162
  25.1 4.0 %reshape_squeeze.7 = bf16[16,128,4,128]{3,2,1,0:T(4,128)(2,1)} reshape(bf16[1,16,128,512]{3,2,1,0:T(8,128)(2,1)} %param.25) | data formatting | bytes 4194304 | tf_op jit(solution)/shard_map/reshape;squeeze | solution.py:163
  30.6 1.3 fusion.85
  32.3 2.3 %fusion.48 = bf16[16,4,8,128]{3,2,1,0:T(8,128)(2,1)S(1)} fusion(bf16[16,128,4,128]{3,2,1,0:T(4,128)(2,1)} %reshape_squeeze.7, f32[16,4,8,128]{3,2,1,0:T(8,128)S(1)} %get-tuple-element.18, f32[16,4,8]{2,1,0:T(4,128)S(1)} %get-tuple-element.12, f32[16,4,128]{2,1,0:T(4,128)S(1)} %reshape.178, f32[16,4,8]{2,1,0:T(4,128)S(1)} %convert_element_type.112, ...), kind=kOutput, calls=%fused_computation.56 | convolution fusion | flops 17170432 | bytes 2529280 | tf_op jit(solution)/shard_map/bkgp,bpkd->bkgd/dot_general | solution.py:180
  34.7 9.1 %all_to_all.63 = bf16[16,4,1024]{2,0,1:T(8,128)(2,1)} all-to-all(bf16[16,4,1024]{2,0,1:T(8,128)(2,1)S(1)} %copy.30), channel_id=1, replica_groups=mesh['grp'=2,'tp'=4,'src'=4] {'tp'}, dimensions={1} | all-to-all | bytes 262144 | tf_op jit(solution)/shard_map/all_to_all | solution.py:624
  43.8 2.1 %split_bytes.3 = bf16[4,64,256]{2,1,0:T(8,128)(2,1)} custom-call(bf16[64,1024]{1,0:T(8,128)(2,1)} %bitcast.68, bf16[512,512]{1,0:T(8,128)(2,1)} %fusion.51.order_ref), custom_call_target="tpu_custom_call" | custom-call | flops 67108864 | bytes 262144 | tf_op jit(solution)/shard_map/split_bytes/pallas_call | solution.py:49
  45.9 3.5 %fusion.13 = f32[64,5120]{1,0:T(8,128)S(1)} fusion(s32[256,5120]{1,0:T(8,128)} %param.27, bf16[4,64,256]{2,1,0:T(8,128)(2,1)} %split_bytes.3), kind=kOutput, calls=%fused_computation.24 | convolution fusion | flops 171704320 | bytes 6586368 | tf_op jit(solution)/shard_map/dot_general | solution.py:63
  49.4 3.5 %convolution_add_fusion.2 = f32[64,5120]{1,0:T(8,128)S(1)} fusion(f32[64,5120]{1,0:T(8,128)S(1)} %fusion.13, s32[256,5120]{1,0:T(8,128)} %param.27, bf16[4,64,256]{2,1,0:T(8,128)(2,1)S(1)} %copy-done.4), kind=kOutput, calls=%fused_computation.6 | convolution fusion | flops 172032000 | bytes 7897088 | tf_op jit(solution)/shard_map/dot_general | solution.py:63
  52.9 0.9 convolution_add_fusion.1
  53.8 0.7 fusion.1
  54.6 0.9 copy.57
  55.5 3.5 %all-to-all-start.2 = ((bf16[64,4,1280]{2,0,1:T(8,128)(2,1)}), bf16[64,4,1280]{2,0,1:T(8,128)(2,1)S(1)}, u32[]{:S(2)}, u32[]{:S(2)}) async-start(bf16[64,4,1280]{2,0,1:T(8,128)(2,1)} %bitcast.59), calls=%async_computation.2 | async-start | bytes 1310720 | tf_op jit(solution)/shard_map/all_to_all | solution.py:196
  59.6 7.1 %all-to-all-done.2 = bf16[64,4,1280]{2,0,1:T(8,128)(2,1)S(1)} async-done(((bf16[64,4,1280]{2,0,1:T(8,128)(2,1)}), bf16[64,4,1280]{2,0,1:T(8,128)(2,1)S(1)}, u32[]{:S(2)}, u32[]{:S(2)}) %all-to-all-start.2) | async-done | bytes 655392 | tf_op jit(solution)/shard_map/all_to_all | solution.py:196
  66.8 1.0 add_convert_fusion.mid_ref
  67.8 11.3 %all_gather.3 = bf16[64,5120]{1,0:T(8,128)(2,1)S(1)} all-gather(bf16[64,1280]{1,0:T(8,128)(2,1)S(1)} %add_convert_fusion.mid_ref), channel_id=1, replica_groups=mesh['grp'=2,'tp'=4,'src'=4] {'tp'}, dimensions={1}, use_global_device_ids=true | all-gather | bytes 819200 | tf_op jit(solution)/shard_map/all_gather | solution.py:630
  80.1 0.9 copy.32
  81.0 4.9 %all-to-all-start.3 = ((bf16[64,4,1280]{2,0,1:T(8,128)(2,1)}), bf16[64,4,1280]{2,0,1:T(8,128)(2,1)S(1)}, u32[]{:S(2)}, u32[]{:S(2)}) async-start(bf16[64,4,1280]{2,0,1:T(8,128)(2,1)} %copy.32), calls=%async_computation.3 | async-start | bytes 1310720 | tf_op jit(solution)/shard_map/all_to_all | solution.py:646
  85.8 0.8 dynamic_slice.15
  88.5 0.8 fusion.58.order_ref
  89.3 9.7 %all-to-all-done.3 = bf16[64,4,1280]{2,0,1:T(8,128)(2,1)S(1)} async-done(((bf16[64,4,1280]{2,0,1:T(8,128)(2,1)}), bf16[64,4,1280]{2,0,1:T(8,128)(2,1)S(1)}, u32[]{:S(2)}, u32[]{:S(2)}) %all-to-all-start.3) | async-done | bytes 655392 | tf_op jit(solution)/shard_map/all_to_all | solution.py:646
  99.0 0.8 copy-done.2
  99.8 83.1 %mlp_block.1 = bf16[64,1280]{1,0:T(8,128)(2,1)} custom-call(bf16[256,1280]{1,0:T(8,128)(2,1)} %bitcast.66, s32[160,3200]{1,0:T(8,128)} %gate_own.1, s32[160,3200]{1,0:T(8,128)} %collective-permute-done.gate_other, s32[160,3200]{1,0:T(8,128)} %up_own.1, s32[160,3200]{1,0:T(8,128)} %collective-permute-done.1.up_other, s32[800,640]{1,0:T(8,128)} %down_own.1, ...), custom_call_target="tpu_custom_call" | custom-call | flops 6291456000 | bytes 12288000 | tf_op jit(solution)/shard_map/mlp_block/pallas_call | solution.py:542
  182.9 1.6 copy.59
  (83 shorter events, 6.2 us)
Async XLA Ops:
  7.9 4.8 %copy-start = (s32[1280,1280]{1,0:T(8,128)S(1)}, s32[1280,1280]{1,0:T(8,128)}, u32[]{:S(2)}) copy-start(s32[1280,1280]{1,0:T(8,128)} %param.20) | copy-start | bytes 19660804
  12.7 2.0 %copy-start.1 = (bf16[4,64,1280]{2,1,0:T(8,128)(2,1)S(1)}, bf16[4,64,1280]{2,1,0:T(8,128)(2,1)}, u32[]{:S(2)}) copy-start(bf16[4,64,1280]{2,1,0:T(8,128)(2,1)} %split_bytes.2) | copy-start | bytes 1966084
  14.8 1.0 copy-start.9
  15.8 6.7 %copy-start.12 = (s32[1,16]{1,0:T(1,128)S(1)}, s32[1,16]{1,0:T(1,128)}, u32[]{:S(2)}) copy-start(s32[1,16]{1,0:T(1,128)} %param.26) | copy-start | bytes 196
  17.3 12.0 %all-to-all-start = ((bf16[4,16,1280]{2,1,0:T(8,128)(2,1)}), bf16[4,16,1280]{2,1,0:T(8,128)(2,1)S(1)}, u32[]{:S(2)}, u32[]{:S(2)}) async-start(bf16[4,16,1280]{2,1,0:T(8,128)(2,1)} %bitcast.5), calls=%async_computation | async-start | bytes 327680 | tf_op jit(solution)/shard_map/all_to_all | solution.py:620
  25.1 4.6 %copy-start.10 = (f32[128]{0:T(128)S(1)}, f32[128]{0:T(128)}, u32[]{:S(2)}) copy-start(f32[128]{0:T(128)} %param.23) | copy-start | bytes 1540
  25.1 4.7 %copy-start.11 = (f32[128]{0:T(128)S(1)}, f32[128]{0:T(128)}, u32[]{:S(2)}) copy-start(f32[128]{0:T(128)} %param.22) | copy-start | bytes 1540
  45.9 3.5 %copy-start.4 = (bf16[4,64,256]{2,1,0:T(8,128)(2,1)S(1)}, bf16[4,64,256]{2,1,0:T(8,128)(2,1)}, u32[]{:S(2)}) copy-start(bf16[4,64,256]{2,1,0:T(8,128)(2,1)} %split_bytes.3) | copy-start | bytes 393220
  45.9 7.0 %slice-start = ((s8[5242880]{0:T(1024)(128)(4,1)}), s8[4194304]{0:T(1024)(128)(4,1)S(1)}, s32[]{:S(2)}) async-start(s8[5242880]{0:T(1024)(128)(4,1)} %bitcast.60), calls=%async_computation.4 | async-start | bytes 8388608
  49.4 3.5 %slice-start.1 = ((s8[5242880]{0:T(1024)(128)(4,1)}), s8[1048576]{0:T(1024)(128)(4,1)S(1)}, s32[]{:S(2)}) async-start(s8[5242880]{0:T(1024)(128)(4,1)} %bitcast.60), calls=%async_computation.5 | async-start | bytes 2097152
  52.9 0.9 copy-start.5
  54.6 4.4 %copy-start.13 = (s32[160,3200]{1,0:T(8,128)S(1)}, s32[160,3200]{1,0:T(8,128)}, u32[]{:S(2)}) copy-start(s32[160,3200]{1,0:T(8,128)} %gate_own.1) | copy-start | bytes 6144004
  54.6 24.7 %copy-start.6 = (f32[5120]{0:T(1024)S(1)}, f32[5120]{0:T(1024)}, u32[]{:S(2)}) copy-start(f32[5120]{0:T(1024)} %param.29) | copy-start | bytes 61444
  55.5 11.2 %all-to-all-start.2 = ((bf16[64,4,1280]{2,0,1:T(8,128)(2,1)}), bf16[64,4,1280]{2,0,1:T(8,128)(2,1)S(1)}, u32[]{:S(2)}, u32[]{:S(2)}) async-start(bf16[64,4,1280]{2,0,1:T(8,128)(2,1)} %bitcast.59), calls=%async_computation.2 | async-start | bytes 1310720 | tf_op jit(solution)/shard_map/all_to_all | solution.py:196
  59.0 40.0 %collective-permute-start = (s32[160,3200]{1,0:T(8,128)S(1)}, s32[160,3200]{1,0:T(8,128)}, u32[]{:S(2)}, u32[]{:S(2)}) collective-permute-start(s32[160,3200]{1,0:T(8,128)S(1)} %copy-done.13), channel_id=1, source_target_pairs={{0,16},{16,0},{1,17},{17,1},{2,18},{18,2},{3,19},{19,3},{4,20},{20... | collective-permute-start | bytes 6144008 | tf_op jit(solution)/shard_map/ppermute | solution.py:637
  59.1 39.9 %collective-permute-start.1 = (s32[160,3200]{1,0:T(8,128)}, s32[160,3200]{1,0:T(8,128)}, u32[]{:S(2)}, u32[]{:S(2)}) collective-permute-start(s32[160,3200]{1,0:T(8,128)} %up_own.1), channel_id=1, source_target_pairs={{0,16},{16,0},{1,17},{17,1},{2,18},{18,2},{3,19},{19,3},{4,20},{20... | collective-permute-start | bytes 6144008 | tf_op jit(solution)/shard_map/ppermute | solution.py:638
  59.6 39.4 %collective-permute-start.2 = (s32[800,640]{1,0:T(8,128)}, s32[800,640]{1,0:T(8,128)}, u32[]{:S(2)}, u32[]{:S(2)}) collective-permute-start(s32[800,640]{1,0:T(8,128)} %down_own.1), channel_id=1, source_target_pairs={{0,16},{16,0},{1,17},{17,1},{2,18},{18,2},{3,19},{19,3},{4,20},{20... | collective-permute-start | bytes 6144008 | tf_op jit(solution)/shard_map/ppermute | solution.py:639
  67.7 12.0 %copy-start.3 = (bf16[64,1280]{1,0:T(8,128)(2,1)}, bf16[64,1280]{1,0:T(8,128)(2,1)S(1)}, u32[]{:S(2)}) copy-start(bf16[64,1280]{1,0:T(8,128)(2,1)S(1)} %add_convert_fusion.mid_ref) | copy-start | bytes 491524
  79.6 7.7 %copy-start.7 = (f32[3200]{0:T(1024)S(1)}, f32[3200]{0:T(1024)}, u32[]{:S(2)}) copy-start(f32[3200]{0:T(1024)} %param.32) | copy-start | bytes 38404
  79.6 8.3 %copy-start.8 = (f32[3200]{0:T(1024)S(1)}, f32[3200]{0:T(1024)}, u32[]{:S(2)}) copy-start(f32[3200]{0:T(1024)} %param.33) | copy-start | bytes 38404
  81.0 18.0 %all-to-all-start.3 = ((bf16[64,4,1280]{2,0,1:T(8,128)(2,1)}), bf16[64,4,1280]{2,0,1:T(8,128)(2,1)S(1)}, u32[]{:S(2)}, u32[]{:S(2)}) async-start(bf16[64,4,1280]{2,0,1:T(8,128)(2,1)} %copy.32), calls=%async_computation.3 | async-start | bytes 1310720 | tf_op jit(solution)/shard_map/all_to_all | solution.py:646
  98.9 0.8 copy-start.2

commit v2 on v1

--- a/solution.py
+++ b/solution.py
@@ -236,69 +236,112 @@
     return jnp.concatenate(parts, axis=0)
 
 
-def mlp_kernel(
-    lag,
-    x_ref,
-    gate_own,
-    gate_other,
-    up_own,
-    up_other,
-    down_own,
-    down_other,
-    gate_scale,
-    up_scale,
-    down_scale,
-    mid_ref,
-    order_ref,
-    out_ref,
-    gate_v,
-    up_v,
-    down_v,
-    x_v,
-    partial,
-    sum_send,
-    sum_recv,
-    act,
-    total,
-    part_send,
-    part_recv,
-    load_sem,
-    sum_send_sem,
-    sum_recv_sem,
-    act_send_sem,
-    act_recv_sem,
-    part_send_sem,
-    part_recv_sem,
-):
-    g, t, s = lax.axis_index("grp"), lax.axis_index("tp"), lax.axis_index("src")
-    count_g, count_t, count_s = lax.axis_size("grp"), lax.axis_size("tp"), lax.axis_size("src")
-    rows = x_ref.shape[0]
-    half = rows // 2
-    packed_rows, hidden = gate_own.shape
-    block = down_own.shape[1]
-    chunks = hidden // LANES
-    groups = load_sem.shape[1]
-    width = hidden // groups
-    per_group = chunks // groups
-    group_rows = rows // count_s
-
-    def load(array, index):
-        source = (gate_own, gate_other, up_own, up_other)[array]
-        target = (gate_v, gate_v, up_v, up_v)[array]
-        columns = pl.ds(pl.multiple_of(index * width, LANES), width)
-        return pltpu.make_async_copy(
-            source.at[:, columns], target.at[array % 2, :, columns], load_sem.at[array, index]
-        )
-
-    def load_down(index):
-        source = (down_own, down_other)[index]
-        return pltpu.make_async_copy(source, down_v.at[index], load_sem.at[4 + index, 0])
-
-    for index in range(groups):
-        for array in range(4):
-            load(array, index).start()
-    for index in range(2):
-        load_down(index).start()
+def stack_lanes(values):
+    blocks = values.shape[1] // LANES
+    return jnp.concatenate([values[:, k * LANES : (k + 1) * LANES] for k in range(blocks)], axis=0)
+
+
+def ordered(stacked, order_ref):
+    return jnp.dot(stacked, order_ref[...], preferred_element_type=jnp.float32).astype(jnp.bfloat16)
+
+
+def row_of(ref):
+    return ref[...].reshape(1, ref.shape[0])
+
+
+def attention_phase(here, inputs, mlp_buffers, scratch, sems):
+    g, t, s, count_g, count_t, count_s = here
+    (
+        hidden_ref,
+        attn_gain,
+        w_qkv,
+        qkv_scale,
+        q_gain,
+        k_gain,
+        keys,
+        values,
+        lengths,
+        w_out,
+        out_scale,
+        mlp_gain,
+        weights,
+        order_ref,
+    ) = inputs
+    gate_v, up_v, down_v, x_v, mid_v = mlp_buffers
+    (
+        qkv_w,
+        out_w,
+        out_u,
+        keys_v,
+        values_v,
+        normed_v,
+        qkv_acc,
+        qkv_send,
+        qkv_recv,
+        q_v,
+        own_v,
+        score_v,
+        own_e_v,
+        denom_v,
+        attn_v,
+        attn_send,
+        attn_recv,
+        proj_v,
+        proj_recv,
+        mid_send,
+        x_send,
+    ) = scratch
+    (
+        qkv_w_sem,
+        out_w_sem,
+        cache_sem,
+        swap_send_sem,
+        swap_recv_sem,
+        load_sem,
+        qkv_send_sem,
+        qkv_recv_sem,
+        attn_send_sem,
+        attn_recv_sem,
+        proj_send_sem,
+        proj_recv_sem,
+        mid_send_sem,
+        mid_recv_sem,
+        z_send_sem,
+        x_send_sem,
+        x_recv_sem,
+    ) = sems
+    f32, bf16 = jnp.float32, jnp.bfloat16
+    rows, model = hidden_ref.shape
+    mine = rows // count_t
+    qkv_columns = w_qkv.shape[1]
+    steps = qkv_w_sem.shape[0]
+    step_rows = w_qkv.shape[0] // steps
+    out_steps = out_w_sem.shape[0]
+    out_width = model // out_steps
+    share = model // count_t
+    positions = keys_v.shape[1]
+    heads = QUERY_HEADS
+    per_kv = QUERY_HEADS // KEY_VALUE_HEADS
+    heads_t = heads // count_t
+
+    def qkv_load(i):
+        part = pl.ds(pl.multiple_of(i * step_rows, step_rows), step_rows)
+        return pltpu.make_async_copy(w_qkv.at[part, :], qkv_w.at[part, :], qkv_w_sem.at[i])
+
+    def out_load(i):
+        part = pl.ds(pl.multiple_of(i * out_width, LANES), out_width)
+        return pltpu.make_async_copy(w_out.at[:, part], out_w.at[:, part], out_w_sem.at[i])
+
+    for i in range(steps):
+        qkv_load(i).start()
+    cache = [
+        pltpu.make_async_copy(keys.at[0], keys_v, cache_sem.at[0]),
+        pltpu.make_async_copy(values.at[0], values_v, cache_sem.at[1]),
+    ]
+    for copy in cache:
+        copy.start()
+    for i in range(out_steps):
+        out_load(i).start()
 
     barrier = pltpu.get_barrier_semaphore()
     for tt in range(count_t):
@@ -310,17 +353,346 @@
                     barrier, inc=1, device_id={"tp": tt, "src": ss}, device_id_type=MESH
                 )
 
+    pl.semaphore_signal(barrier, inc=1, device_id={"grp": 1 - g}, device_id_type=MESH)
+
+    normed = normalize_rows(hidden_ref[...].astype(f32), row_of(attn_gain)).astype(bf16)
+    moved = ordered(stack_lanes(normed), order_ref)
+    for k in range(model // LANES):
+        normed_v[:, k * LANES : (k + 1) * LANES] = moved[k * rows : (k + 1) * rows]
+    pl.semaphore_wait(barrier, count_t * count_s)
+
+    swaps = [
+        pltpu.make_async_remote_copy(
+            src_ref=source,
+            dst_ref=target.at[1],
+            send_sem=swap_send_sem.at[index],
+            recv_sem=swap_recv_sem.at[index],
+            device_id={"grp": 1 - g},
+            device_id_type=MESH,
+        )
+        for index, (source, target) in enumerate(zip(weights, (gate_v, up_v, down_v)))
+    ]
+    loads = [
+        pltpu.make_async_copy(source, target.at[0], load_sem.at[index])
+        for index, (source, target) in enumerate(zip(weights, (gate_v, up_v, down_v)))
+    ]
+
+    qkv_acc[...] = jnp.zeros_like(qkv_acc)
+
+    def qkv_step(i, carry):
+        qkv_load(i).wait()
+        part = pl.ds(pl.multiple_of(i * step_rows, step_rows), step_rows)
+        depth = pl.ds(pl.multiple_of(i * 4 * step_rows, LANES), 4 * step_rows)
+        qkv_acc[...] += jnp.dot(
+            normed_v[:, depth], unpack_slab(qkv_w[part, :]), preferred_element_type=f32
+        )
+        return carry
+
+    lax.fori_loop(0, steps, qkv_step, 0)
+    for copy in swaps + loads:
+        copy.start()
+    qkv_send[...] = (qkv_acc[...] * row_of(qkv_scale)).astype(bf16)
+
+    def peer_of(shift):
+        return lax.rem(t + shift, count_t)
+
+    def rows_of(index):
+        return pl.ds(pl.multiple_of(index * mine, mine), mine)
+
+    def qkv_copy(peer, slot):
+        return pltpu.make_async_remote_copy(
+            src_ref=qkv_send.at[rows_of(peer), :],
+            dst_ref=qkv_recv.at[slot],
+            send_sem=qkv_send_sem.at[peer],
+            recv_sem=qkv_recv_sem.at[slot],
+            device_id={"tp": peer},
+            device_id_type=MESH,
+        )
+
+    for shift in range(1, count_t):
+        qkv_copy(peer_of(shift), t).start()
+    qkv_recv[t] = qkv_send[rows_of(t), :]
+
+    def unpack_out(i, carry):
+        out_load(i).wait()
+        part = pl.ds(pl.multiple_of(i * out_width, LANES), out_width)
+        out_u[:, part] = unpack_slab(out_w[:, part])
+        return carry
+
+    lax.fori_loop(0, out_steps, unpack_out, 0)
+
+    row_index = lax.broadcasted_iota(jnp.int32, (mine, HEAD_SIZE), 0)
+    lane = lax.broadcasted_iota(jnp.int32, (mine, HEAD_SIZE), 1)
+    place = jnp.zeros((mine, HEAD_SIZE), f32)
+    for b in range(mine):
+        place = jnp.where(row_index == b, lengths[0, b].astype(f32), place)
+    half_dim = HEAD_SIZE // 2
+    low = lane < half_dim
+    frequency = jnp.where(low, lane, lane - half_dim).astype(f32)
+    angle = place * jnp.exp(frequency * (-math.log(rope_base) / half_dim))
+    cosine = jnp.cos(angle)
+    sine = jnp.sin(angle)
+    sine = jnp.where(low, -sine, sine)
+
+    for shift in range(1, count_t):
+        qkv_copy(t, peer_of(shift)).wait_recv()
+
+    per_share = qkv_columns // HEAD_SIZE
+
+    def head_of(h):
+        column = (h % per_share) * HEAD_SIZE
+        return qkv_recv[h // per_share, :, column : column + HEAD_SIZE]
+
+    def turned(h, gain):
+        value = normalize_rows(head_of(h).astype(f32), gain)
+        other = pltpu.roll(value, half_dim, 1)
+        return (value * cosine + other * sine).astype(bf16).astype(f32)
+
+    logit_scale = 1.0 / math.sqrt(HEAD_SIZE)
+    q_row, k_row = row_of(q_gain), row_of(k_gain)
+    for kv in range(KEY_VALUE_HEADS):
+        new_key = turned(heads + kv, k_row)
+        for h in range(kv * per_kv, (kv + 1) * per_kv):
+            query = turned(h, q_row)
+            q_v[h * mine : (h + 1) * mine] = query
+            own = jnp.sum(query * new_key, axis=1, keepdims=True) * logit_scale
+            own_v[h * mine : (h + 1) * mine] = jnp.broadcast_to(own, (mine, HEAD_SIZE))
+    for copy in cache:
+        copy.wait()
+
+    zeros = jnp.zeros((per_kv, HEAD_SIZE), f32)
+    for b in range(mine):
+        query = q_v[pl.ds(b, heads, stride=mine), :]
+        spread = jnp.concatenate(
+            [
+                jnp.concatenate(
+                    [
+                        query[kv * per_kv : (kv + 1) * per_kv] if kv == place_of else zeros
+                        for place_of in range(KEY_VALUE_HEADS)
+                    ],
+                    axis=1,
+                )
+                for kv in range(KEY_VALUE_HEADS)
+            ],
+            axis=0,
+        ).astype(bf16)
+        score_v[b * heads : (b + 1) * heads] = lax.dot_general(
+            spread, keys_v[b], (((1,), (1,)), ((), ())), preferred_element_type=f32
+        )
+    position = lax.broadcasted_iota(jnp.int32, (heads, positions), 1)
+    for b in range(mine):
+        strided = pl.ds(b, heads, stride=mine)
+        scores = score_v[b * heads : (b + 1) * heads] * logit_scale
+        scores = jnp.where(position < lengths[0, b], scores, -jnp.inf)
+        own = own_v[strided, :][:, :1]
+        top = jnp.maximum(jnp.max(scores, axis=1, keepdims=True), own)
+        weight = jnp.exp(scores - top)
+        own_e = jnp.exp(own - top)
+        denominator = jnp.sum(weight, axis=1, keepdims=True) + own_e
+        score_v[b * heads : (b + 1) * heads] = weight
+        own_e_v[strided, :] = jnp.broadcast_to(own_e, (heads, HEAD_SIZE))
+        denom_v[strided, :] = jnp.broadcast_to(denominator, (heads, HEAD_SIZE))
+    for b in range(mine):
+        mixed = jnp.dot(
+            score_v[b * heads : (b + 1) * heads].astype(bf16),
+            values_v[b],
+            preferred_element_type=f32,
+        )
+        attn_v[pl.ds(b, heads, stride=mine), :] = jnp.concatenate(
+            [
+                mixed[kv * per_kv : (kv + 1) * per_kv, kv * HEAD_SIZE : (kv + 1) * HEAD_SIZE]
+                for kv in range(KEY_VALUE_HEADS)
+            ],
+            axis=0,
+        )
+    finished = []
+    for h in range(heads):
+        part = slice(h * mine, (h + 1) * mine)
+        new_value = head_of(heads + KEY_VALUE_HEADS + h // per_kv).astype(f32)
+        own_low = own_e_v[part].astype(bf16).astype(f32)
+        finished.append(((attn_v[part] + own_low * new_value) / denom_v[part]).astype(bf16))
+    attn_send[...] = ordered(jnp.concatenate(finished, axis=0), order_ref)
+
+    head_rows = heads_t * mine
+
+    def attn_copy(peer, slot):
+        return pltpu.make_async_remote_copy(
+            src_ref=attn_send.at[pl.ds(pl.multiple_of(peer * head_rows, head_rows), head_rows), :],
+            dst_ref=attn_recv.at[slot],
+            send_sem=attn_send_sem.at[peer],
+            recv_sem=attn_recv_sem.at[slot],
+            device_id={"tp": peer},
+            device_id_type=MESH,
+        )
+
+    for shift in range(1, count_t):
+        attn_copy(peer_of(shift), t).start()
+    attn_recv[t] = attn_send[pl.ds(pl.multiple_of(t * head_rows, head_rows), head_rows), :]
+    for shift in range(1, count_t):
+        attn_copy(t, peer_of(shift)).wait_recv()
+
+    def proj_copy(peer, slot, i):
+        part = pl.ds(pl.multiple_of(i * out_width, LANES), out_width)
+        return pltpu.make_async_remote_copy(
+            src_ref=proj_v.at[rows_of(peer), part],
+            dst_ref=proj_recv.at[slot, :, part],
+            send_sem=proj_send_sem.at[peer, i],
+            recv_sem=proj_recv_sem.at[slot, i],
+            device_id={"tp": peer},
+            device_id_type=MESH,
+        )
+
+    def out_step(i, carry):
+        part = pl.ds(pl.multiple_of(i * out_width, LANES), out_width)
+        left = jnp.concatenate(
+            [
+                jnp.concatenate(
+                    [attn_recv[tt, h * mine : (h + 1) * mine] for tt in range(count_t)], axis=0
+                )
+                for h in range(heads_t)
+            ],
+            axis=1,
+        )
+        product = jnp.dot(left, out_u[:, part], preferred_element_type=f32)
+        proj_v[:, part] = (product * out_scale[part].reshape(1, out_width)).astype(bf16)
+        for shift in range(1, count_t):
+            proj_copy(peer_of(shift), t, i).start()
+        return carry
+
+    lax.fori_loop(0, out_steps, out_step, 0)
+
+    total = hidden_ref[rows_of(t), :].astype(f32) + proj_v[rows_of(t), :].astype(f32)
+    for shift in range(1, count_t):
+        slot = peer_of(shift)
+
+        def wait_part(i, carry):
+            proj_copy(t, slot, i).wait_recv()
+            return carry
+
+        lax.fori_loop(0, out_steps, wait_part, 0)
+        total += proj_recv[slot].astype(f32)
+    mid = total.astype(bf16)
+    for tt in range(count_t):
+        mid_send[tt] = mid[:, tt * share : (tt + 1) * share]
+    moved = ordered(
+        stack_lanes(normalize_rows(mid.astype(f32), row_of(mlp_gain)).astype(bf16)), order_ref
+    )
+    block = model // (count_g * count_s) // LANES
+    for number in range(count_g * count_s):
+        owner = number % count_s
+        first = jnp.where(number // count_s == g, 0, block)
+        for k in range(block):
+            column = pl.multiple_of((first + k) * LANES, LANES)
+            source = number * block + k
+            x_send[owner, :, pl.ds(column, LANES)] = moved[source * mine : (source + 1) * mine]
+
+    def x_rows(ss, tt):
+        return pl.ds(pl.multiple_of((ss * count_t + tt) * mine, mine), mine)
+
+    def z_copy(peer, ss):
+        return pltpu.make_async_remote_copy(
+            src_ref=x_send.at[peer],
+            dst_ref=x_v.at[x_rows(ss, t), :],
+            send_sem=z_send_sem.at[peer],
+            recv_sem=x_recv_sem.at[ss, t],
+            device_id={"src": peer},
+            device_id_type=MESH,
+        )
+
+    def x_copy(peer, ss, tt):
+        return pltpu.make_async_remote_copy(
+            src_ref=x_v.at[x_rows(ss, tt), :],
+            dst_ref=x_v.at[x_rows(ss, tt), :],
+            send_sem=x_send_sem.at[ss, peer],
+            recv_sem=x_recv_sem.at[ss, tt],
+            device_id={"tp": peer},
+            device_id_type=MESH,
+        )
+
+    def own_copy(peer):
+        return pltpu.make_async_remote_copy(
+            src_ref=x_send.at[s],
+            dst_ref=x_v.at[x_rows(s, t), :],
+            send_sem=x_send_sem.at[s, peer],
+            recv_sem=x_recv_sem.at[s, t],
+            device_id={"tp": peer},
+            device_id_type=MESH,
+        )
+
+    def mid_copy(peer, slot):
+        return pltpu.make_async_remote_copy(
+            src_ref=mid_send.at[peer],
+            dst_ref=mid_v.at[rows_of(slot), :],
+            send_sem=mid_send_sem.at[peer],
+            recv_sem=mid_recv_sem.at[slot],
+            device_id={"tp": peer},
+            device_id_type=MESH,
+        )
+
+    for shift in range(1, count_s):
+        z_copy(lax.rem(s + shift, count_s), s).start()
+    for shift in range(1, count_t):
+        own_copy(peer_of(shift)).start()
+    x_v[x_rows(s, t), :] = x_send[s]
+    for shift in range(1, count_s):
+        ss = lax.rem(s + shift, count_s)
+        z_copy(s, ss).wait_recv()
+        for turn in range(1, count_t):
+            x_copy(peer_of(turn), ss, t).start()
+    for shift in range(1, count_t):
+        mid_copy(peer_of(shift), t).start()
+    mid_v[rows_of(t), :] = mid_send[t]
+    for ss in range(count_s):
+        for turn in range(1, count_t):
+            x_copy(t, ss, peer_of(turn)).wait_recv()
+
+    def finish():
+        for shift in range(1, count_t):
+            peer = peer_of(shift)
+            qkv_copy(peer, t).wait_send()
+            attn_copy(peer, t).wait_send()
+            mid_copy(peer, t).wait_send()
+
+            def wait_part(i, carry):
+                proj_copy(peer, t, i).wait_send()
+                return carry
+
+            lax.fori_loop(0, out_steps, wait_part, 0)
+            for ss in range(count_s):
+                x_copy(peer, ss, t).wait_send()
+        for shift in range(1, count_s):
+            z_copy(lax.rem(s + shift, count_s), s).wait_send()
+        for copy in swaps:
+            copy.wait_send()
+
+    def mid_wait():
+        for shift in range(1, count_t):
+            mid_copy(t, peer_of(shift)).wait_recv()
+
+    return swaps, loads, mid_wait, finish
+
+
+def mlp_phase(here, lag, scales, mlp_buffers, scratch, sems, attention, out_ref):
+    g, t, s, count_g, count_t, count_s = here
+    gate_scale, up_scale, down_scale, order_ref = scales
+    gate_v, up_v, down_v, x_v, mid_v = mlp_buffers
+    partial, sum_recv, act, total, part_send, part_recv = scratch
+    (
+        sum_send_sem,
+        sum_recv_sem,
+        act_send_sem,
+        act_recv_sem,
+        part_send_sem,
+        part_recv_sem,
+    ) = sems
+    swaps, loads, mid_wait, finish = attention
+    rows = x_v.shape[0]
+    half = rows // 2
+    hidden = gate_v.shape[2]
+    block = down_v.shape[2]
+    chunks = hidden // LANES
+    group_rows = rows // count_s
     total[...] = jnp.zeros_like(total)
-    blocks = x_ref.shape[1] // LANES
-    stacked = jnp.concatenate(
-        [x_ref[:, k * LANES : (k + 1) * LANES] for k in range(blocks)], axis=0
-    )
-    moved = jnp.dot(stacked, order_ref[...], preferred_element_type=jnp.float32).astype(
-        jnp.bfloat16
-    )
-    for k in range(blocks):
-        x_v[:, k * LANES : (k + 1) * LANES] = moved[k * rows : (k + 1) * rows]
-    pl.semaphore_wait(barrier, count_t * count_s - 1)
 
     last = count_s - 1
     far = last * lag
@@ -328,7 +700,7 @@
 
     def sum_copy(side, j):
         return pltpu.make_async_remote_copy(
-            src_ref=sum_send.at[side, j],
+            src_ref=partial.at[j, side],
             dst_ref=sum_recv.at[side, j],
             send_sem=sum_send_sem.at[side, j],
             recv_sem=sum_recv_sem.at[side, j],
@@ -359,22 +731,21 @@
 
         @pl.when(depth == 0)
         def _():
-            sum_send[side, j] = partial[j, side].astype(jnp.bfloat16)
             sum_copy(side, j).start()
 
         @pl.when((depth > 0) & jnp.logical_not(at_end))
         def _():
-            sum_send[side, j] = (
-                partial[j, side] + sum_recv[side, j].astype(jnp.float32)
+            partial[j, side] = (
+                partial[j, side].astype(jnp.float32) + sum_recv[side, j].astype(jnp.float32)
             ).astype(jnp.bfloat16)
             sum_copy(side, j).start()
 
         @pl.when(at_end)
         def _():
-            value = partial[j, side] + sum_recv[side, j].astype(jnp.float32)
+            value = partial[j, side].astype(jnp.float32) + sum_recv[side, j].astype(jnp.float32)
             columns = pl.ds(pl.multiple_of(j * LANES, LANES), LANES)
-            gate_value = value[:, :LANES] * gate_scale[:, columns]
-            up_value = value[:, LANES:] * up_scale[:, columns]
+            gate_value = value[:, :LANES] * gate_scale[columns].reshape(1, LANES)
+            up_value = value[:, LANES:] * up_scale[columns].reshape(1, LANES)
             activated = (gate_value / (1.0 + jnp.exp(-gate_value)) * up_value).astype(jnp.bfloat16)
             act[j, side] = jnp.dot(
                 activated, order_ref[...], preferred_element_type=jnp.float32
@@ -392,10 +763,11 @@
     def step(i, carry):
         @pl.when(i < chunks)
         def _():
-            @pl.when(lax.rem(i, per_group) == 0)
+            @pl.when(i == 0)
             def _():
-                for array in range(4):
-                    load(array, i // per_group).wait()
+                for index in range(2):
+                    loads[index].wait()
+                    swaps[index].wait_recv()
 
             columns = pl.ds(pl.multiple_of(i * LANES, LANES), LANES)
             gate_w = [unpack_slab(gate_v[index, :, columns]) for index in range(2)]
@@ -404,6 +776,7 @@
                 [jnp.concatenate(gate_w, axis=0), jnp.concatenate(up_w, axis=0)], axis=1
             )
             product = jnp.dot(x_v[...], weights, preferred_element_type=jnp.float32)
+            product = product.astype(jnp.bfloat16)
             partial[i, 0] = product[:half]
             partial[i, 1] = product[half:]
 
@@ -428,8 +801,8 @@
         def _():
             @pl.when(j == 0)
             def _():
-                for index in range(2):
-                    load_down(index).wait()
+                loads[2].wait()
+                swaps[2].wait_recv()
 
             slab = LANES // 4
             words = pl.ds(pl.multiple_of(j * slab, slab), slab)
@@ -492,13 +865,15 @@
                 device_id_type=MESH,
             ).wait_recv()
 
+    mid_wait()
     for place in range(per_share):
         value = part_recv[place].astype(jnp.float32)
         for tt in range(1, count_t):
             value += part_recv[tt * per_share + place].astype(jnp.float32)
         columns = slice(place * block, (place + 1) * block)
+        scale_at = pl.ds(pl.multiple_of((t * per_share + place) * block, LANES), block)
         out_ref[:, columns] = (
-            mid_ref[:, columns].astype(jnp.float32) + value * down_scale[:, columns]
+            mid_v[:, columns].astype(jnp.float32) + value * down_scale[scale_at].reshape(1, block)
         ).astype(jnp.bfloat16)
 
     for ss in range(count_s):
@@ -524,70 +899,229 @@
         return carry
 
     lax.fori_loop(0, chunks, drain, 0)
-
-
-def mlp_block(x, gate, up, down, gate_scale, up_scale, down_scale, mid, lag):
-    count_t, count_s = lax.axis_size("tp"), lax.axis_size("src")
-    rows, depth = x.shape
-    packed_rows, hidden = gate[0].shape
-    packed_hidden, block = down[0].shape
+    finish()
+
+
+def layer_kernel(lag, counts, *refs):
+    count_in, count_buffers, count_a, count_asem, count_b, count_bsem = counts
+    take = iter(refs)
+
+    def some(count):
+        return [next(take) for _ in range(count)]
+
+    (
+        hidden_ref,
+        attn_gain,
+        w_qkv,
+        qkv_scale,
+        q_gain,
+        k_gain,
+        keys,
+        values,
+        lengths,
+        w_out,
+        out_scale,
+        mlp_gain,
+        w_gate,
+        w_up,
+        gate_scale,
+        up_scale,
+        w_down,
+        down_scale,
+        order_ref,
+    ) = some(count_in)
+    out_ref = next(take)
+    mlp_buffers = some(count_buffers)
+    scratch_a, sems_a = some(count_a), some(count_asem)
+    scratch_b, sems_b = some(count_b), some(count_bsem)
+    here = tuple(lax.axis_index(name) for name in ("grp", "tp", "src")) + tuple(
+        lax.axis_size(name) for name in ("grp", "tp", "src")
+    )
+    attention = attention_phase(
+        here,
+        (
+            hidden_ref,
+            attn_gain,
+            w_qkv,
+            qkv_scale,
+            q_gain,
+            k_gain,
+            keys,
+            values,
+            lengths,
+            w_out,
+            out_scale,
+            mlp_gain,
+            (w_gate, w_up, w_down),
+            order_ref,
+        ),
+        mlp_buffers,
+        scratch_a,
+        sems_a,
+    )
+    mlp_phase(
+        here,
+        lag,
+        (gate_scale, up_scale, down_scale, order_ref),
+        mlp_buffers,
+        scratch_b,
+        sems_b,
+        attention,
+        out_ref,
+    )
+
+
+def layer(args, lag):
+    (
+        hidden_in,
+        attn_gain,
+        w_qkv,
+        qkv_scale,
+        q_gain,
+        k_gain,
+        key_cache,
+        value_cache,
+        lengths,
+        w_out,
+        out_scale,
+        mlp_gain,
+        w_gate,
+        w_up,
+        gate_scale,
+        up_scale,
+        w_down,
+        down_scale,
+    ) = args
+    count_g, count_t, count_s = (lax.axis_size(name) for name in ("grp", "tp", "src"))
+    group_rows, model = hidden_in.shape
+    rows = group_rows * count_s
+    half = rows // 2
+    mine = group_rows // count_t
+    packed_rows, hidden = w_gate.shape
+    packed_hidden, block = w_down.shape
+    depth = 2 * block
     chunks = hidden // LANES
-    groups = 5 if chunks % 5 == 0 else 1
-    half = rows // 2
-    group_rows = rows // count_s
-    slots = count_t * (mid.shape[1] // block)
-    bf16, f32 = jnp.bfloat16, jnp.float32
+    share = model // count_t
+    slots = count_g * count_s
+    steps = 10 if w_qkv.shape[0] % 320 == 0 else w_qkv.shape[0] // 32
+    out_steps = 10 if model % (10 * LANES) == 0 else model // LANES
+    qkv_columns = w_qkv.shape[1]
+    head_rows = QUERY_HEADS * mine
+    bf16, f32, i32 = jnp.bfloat16, jnp.float32, jnp.int32
+    dma = pltpu.SemaphoreType.DMA
     vmem = pl.BlockSpec(memory_space=pltpu.VMEM)
+    smem = pl.BlockSpec(memory_space=pltpu.SMEM)
     hbm = pl.BlockSpec(memory_space=pl.ANY)
+    buffers = [
+        pltpu.VMEM((2, packed_rows, hidden), i32),
+        pltpu.VMEM((2, packed_rows, hidden), i32),
+        pltpu.VMEM((2, packed_hidden, block), i32),
+        pltpu.VMEM((rows, depth), bf16),
+        pltpu.VMEM((group_rows, share), bf16),
+    ]
+    scratch_a = [
+        pltpu.VMEM(w_qkv.shape, i32),
+        pltpu.VMEM(w_out.shape, i32),
+        pltpu.VMEM((4 * w_out.shape[0], model), bf16),
+        pltpu.VMEM(key_cache.shape[1:], bf16),
+        pltpu.VMEM(value_cache.shape[1:], bf16),
+        pltpu.VMEM((group_rows, model), bf16),
+        pltpu.VMEM((group_rows, qkv_columns), f32),
+        pltpu.VMEM((group_rows, qkv_columns), bf16),
+        pltpu.VMEM((count_t, mine, qkv_columns), bf16),
+        pltpu.VMEM((head_rows, HEAD_SIZE), f32),
+        pltpu.VMEM((head_rows, HEAD_SIZE), f32),
+        pltpu.VMEM((head_rows, key_cache.shape[2]), f32),
+        pltpu.VMEM((head_rows, HEAD_SIZE), f32),
+        pltpu.VMEM((head_rows, HEAD_SIZE), f32),
+        pltpu.VMEM((head_rows, HEAD_SIZE), f32),
+        pltpu.VMEM((head_rows, HEAD_SIZE), bf16),
+        pltpu.VMEM((count_t, head_rows // count_t, HEAD_SIZE), bf16),
+        pltpu.VMEM((group_rows, model), bf16),
+        pltpu.VMEM((count_t, mine, model), bf16),
+        pltpu.VMEM((count_t, mine, share), bf16),
+        pltpu.VMEM((count_s, mine, depth), bf16),
+    ]
+    sems_a = [
+        dma((steps,)),
+        dma((out_steps,)),
+        dma((2,)),
+        dma((3,)),
+        dma((3,)),
+        dma((3,)),
+        dma((count_t,)),
+        dma((count_t,)),
+        dma((count_t,)),
+        dma((count_t,)),
+        dma((count_t, out_steps)),
+        dma((count_t, out_steps)),
+        dma((count_t,)),
+        dma((count_t,)),
+        dma((count_s,)),
+        dma((count_s, count_t)),
+        dma((count_s, count_t)),
+    ]
+    scratch_b = [
+        pltpu.VMEM((chunks, 2, half, 2 * LANES), bf16),
+        pltpu.VMEM((2, chunks, half, 2 * LANES), bf16),
+        pltpu.VMEM((chunks, 2, half, LANES), bf16),
+        pltpu.VMEM((rows, depth), f32),
+        pltpu.VMEM((2, count_s, group_rows, block), bf16),
+        pltpu.VMEM((slots, group_rows, block), bf16),
+    ]
+    sems_b = [
+        dma((2, chunks)),
+        dma((2, chunks)),
+        dma((2, chunks)),
+        dma((2, chunks)),
+        dma((2, count_s)),
+        dma((slots,)),
+    ]
+    specs = [vmem] * (len(args) + 1)
+    for place in (2, 6, 7, 9, 12, 13, 16):
+        specs[place] = hbm
+    specs[8] = smem
+    counts = (
+        len(specs),
+        len(buffers),
+        len(scratch_a),
+        len(sems_a),
+        len(scratch_b),
+        len(sems_b),
+    )
     return pl.pallas_call(
-        functools.partial(mlp_kernel, lag),
-        out_shape=jax.ShapeDtypeStruct(mid.shape, bf16),
-        in_specs=[vmem] + [hbm] * 6 + [vmem] * 5,
+        functools.partial(layer_kernel, lag, counts),
+        out_shape=jax.ShapeDtypeStruct((group_rows, share), bf16),
+        in_specs=specs,
         out_specs=vmem,
-        scratch_shapes=[
-            pltpu.VMEM((2, packed_rows, hidden), jnp.int32),
-            pltpu.VMEM((2, packed_rows, hidden), jnp.int32),
-            pltpu.VMEM((2, packed_hidden, block), jnp.int32),
-            pltpu.VMEM((rows, depth), bf16),
-            pltpu.VMEM((chunks, 2, half, 2 * LANES), f32),
-            pltpu.VMEM((2, chunks, half, 2 * LANES), bf16),
-            pltpu.VMEM((2, chunks, half, 2 * LANES), bf16),
-            pltpu.VMEM((chunks, 2, half, LANES), bf16),
-            pltpu.VMEM((rows, depth), f32),
-            pltpu.VMEM((2, count_s, group_rows, block), bf16),
-            pltpu.VMEM((slots, group_rows, block), bf16),
-            pltpu.SemaphoreType.DMA((6, groups)),
-            pltpu.SemaphoreType.DMA((2, chunks)),
-            pltpu.SemaphoreType.DMA((2, chunks)),
-            pltpu.SemaphoreType.DMA((2, chunks)),
-            pltpu.SemaphoreType.DMA((2, chunks)),
-            pltpu.SemaphoreType.DMA((2, count_s)),
-            pltpu.SemaphoreType.DMA((slots,)),
-        ],
+        scratch_shapes=buffers + scratch_a + sems_a + scratch_b + sems_b,
         compiler_params=pltpu.CompilerParams(
-            collective_id=1, has_side_effects=True, vmem_limit_bytes=56 * 1024 * 1024
+            collective_id=1, has_side_effects=True, vmem_limit_bytes=63 * 1024 * 1024
         ),
-        cost_estimate=pl.CostEstimate(
-            flops=2 * rows * depth * hidden * 3,
-            bytes_accessed=4 * 3 * 2 * packed_rows * hidden,
-            transcendentals=rows * hidden,
-        ),
-        name="mlp_block",
-    )(x, *gate, *up, *down, gate_scale, up_scale, down_scale, mid, lane_order(LANES))
-
-
-def fast_mlp(grp, tp, src, args):
-    w_gate, w_down, hidden_in = args
-    rows = hidden_in.shape[0]
+        name="layer",
+    )(*args, lane_order(LANES))
+
+
+def fast_layer(args):
+    hidden_in, w_qkv, w_out, w_gate, w_down = (args[k] for k in (0, 2, 9, 12, 16))
+    grp, tp, src = (lax.axis_size(name) for name in ("grp", "tp", "src"))
+    rows, model = hidden_in.shape
     return (
         grp == 2
         and src > 1
+        and tp > 1
         and (grp * src) % tp == 0
+        and rows % (16 * tp) == 0
+        and QUERY_HEADS % tp == 0
+        and model % (LANES * tp) == 0
+        and w_qkv.shape[0] % 32 == 0
+        and w_qkv.shape[1] % HEAD_SIZE == 0
+        and w_out.shape[0] % 32 == 0
         and w_gate.shape[0] % 32 == 0
         and w_gate.shape[1] % LANES == 0
         and w_down.shape[1] % LANES == 0
-        and rows % 16 == 0
-        and (rows * src) % 32 == 0
+        and args[6].shape[2] == LANES
+        and HEAD_SIZE == LANES
     )
 
 
@@ -611,6 +1145,28 @@
     w_down,
     down_scale,
 ):
+    args = (
+        hidden_in,
+        attn_gain,
+        w_qkv,
+        qkv_scale,
+        q_gain,
+        k_gain,
+        key_cache,
+        value_cache,
+        lengths,
+        w_out,
+        out_scale,
+        mlp_gain,
+        w_gate,
+        w_up,
+        gate_scale,
+        up_scale,
+        w_down,
+        down_scale,
+    )
+    if fast_layer(args):
+        return layer(args, 2)
     tp_count = lax.axis_size("tp")
     tp_index = lax.axis_index("tp")
     share_cols = D // tp_count
@@ -629,34 +1185,6 @@
     ).astype(jnp.bfloat16)
     mid_full = lax.all_gather(mid_share, "tp", axis=1, tiled=True)
     normed_mlp = normalize_rows(mid_full.astype(jnp.float32), mlp_gain).astype(jnp.bfloat16)
-    if fast_mlp(lax.axis_size("grp"), tp_count, lax.axis_size("src"), (w_gate, w_down, hidden_in)):
-        g = lax.axis_index("grp")
-        count_s = lax.axis_size("src")
-        rows = hidden_in.shape[0]
-        swap = [(0, 1), (1, 0)]
-        gate = (w_gate, lax.ppermute(w_gate, "grp", swap))
-        up = (w_up, lax.ppermute(w_up, "grp", swap))
-        down = (w_down, lax.ppermute(w_down, "grp", swap))
-        width = D // 2
-        own = lax.dynamic_slice_in_dim(normed_mlp, g * width, width, 1)
-        other = lax.dynamic_slice_in_dim(normed_mlp, (1 - g) * width, width, 1)
-        both = jnp.concatenate(
-            [own.reshape(rows, count_s, -1), other.reshape(rows, count_s, -1)], axis=2
-        )
-        x = lax.all_to_all(both, "src", split_axis=1, concat_axis=0, tiled=True)
-        x = x.reshape(rows * count_s, -1)
-        down_share = lax.dynamic_slice_in_dim(down_scale, tp_index * share_cols, share_cols, 0)
-        return mlp_block(
-            x,
-            gate,
-            up,
-            down,
-            gate_scale[None],
-            up_scale[None],
-            down_share[None],
-            mid_share,
-            2,
-        )
     mlp_columns = order_bytes(
         lax.all_to_all(normed_mlp, ("grp", "src"), split_axis=1, concat_axis=0, tiled=True)
     )

time: 185 us -> 129 us (0.70)
  Pallas kernels: 88.3 us -> 125 us
  matrix products: 21.1 us -> 0 us
  blocking collectives: 20.4 us -> 0 us
  waiting for transfers between devices: 16.7 us -> 0 us
  starting transfers between devices: 14.2 us -> 0 us
  local copies, waits for them, and re-layouts: 14.5 us -> 1.59 us
  other arithmetic: 8.75 us -> 0.8 us
    pallas_call x3 -> x1, Pallas kernels: 88.3 us -> 125 us  [layer(): pl.pallas_call(functools.partial(layer_kernel, lag, counts), out_shape=ja...]
    dot_general x11 -> x0, matrix products: 21.1 us -> none  [the longest x8 17.2 us: byte_product(): jnp.dot(pieces[byte_index], unpack_bytes(packed, byte_index).astype(jnp.b...]
    all_to_all x3 -> x0, waiting for transfers between devices: 16.7 us -> none  [the longest x1 9.68 us: local(): x = lax.all_to_all(both, 'src', split_axis=1, concat_axis=0, tiled=True)]
    all_to_all x3 -> x0, starting transfers between devices: 13.6 us -> none  [the longest x1 5.2 us: local(): lax.all_to_all(qkv_part, 'tp', split_axis=0, concat_axis=1, tiled=True)]
    all_gather x1 -> x0, blocking collectives: 11.3 us -> none  [local(): mid_full = lax.all_gather(mid_share, 'tp', axis=1, tiled=True)]
    all_to_all x1 -> x0, blocking collectives: 9.11 us -> none  [local(): lax.all_to_all(heads_out, 'tp', split_axis=1, concat_axis=0, tiled=True)]
    another operation x2 -> x0, local copies, waits for them, and re-layouts: 6.56 us -> none  [the longest x1 4 us: local_attention(): stored_values.reshape(count_of_rows, cache_length, KEY_VALUE_HEADS, HEAD_...]
    convert_element_type x8 -> x0, other arithmetic: 4.68 us -> none  [the longest x1 2.17 us: local(): normed = normalize_rows(residual, attn_gain).astype(jnp.bfloat16)]
  transfers between devices with their start and end apart: 6 -> 0, of which waited for: 2 -> 0; matrix products, arithmetic and copies ran while one was open for 7% -> 0% of each run, Pallas kernels for 0% -> 0%
where the time goes in v2:
time: 129 us; the launch traced here: 128 us
  Pallas kernels  125 us (97%)
  local copies, waits for them, and re-layouts  1.59 us (1%)
    pallas_call x1, Pallas kernels, layer(): pl.pallas_call(functools.partial(layer_kernel, lag, counts), out_shape=ja...  125 us

profile of v2, /device:TPU:0, one launch (start us, length us, event | category | flops | bytes accessed | tf_op | source)
XLA Modules:
  0.0 127.7 jit_solution(16290424498306307437)
XLA Ops:
  0.0 0.8 fusion.refs_18_
  0.8 125.3 %layer.1 = bf16[64,1280]{1,0:T(8,128)(2,1)} custom-call(bf16[64,5120]{1,0:T(8,128)(2,1)} %refs_0_.1, f32[5120]{0:T(1024)} %refs_1_.1, s32[1280,1280]{1,0:T(8,128)} %refs_2_.1, f32[1280]{0:T(1024)} %refs_3_.1, f32[128]{0:T(128)} %refs_4_.1, f32[128]{0:T(128)} %refs_5_.1, bf16[1,16,128,512]{3,2,1,0:T(8,128)(2,1)} %refs_6_.1, ...), custom_call_target="tpu_custom_call" | custom-call | tf_op jit(solution)/shard_map/layer/pallas_call | solution.py:1092
  126.1 1.6 %copy.20 = bf16[64,1280]{1,0:T(8,128)(2,1)} copy(bf16[64,1280]{1,0:T(8,128)(2,1)} %layer.1) | data formatting | bytes 327680
  (3 shorter events, 0.0 us)

commit v3 on v2

--- a/solution.py
+++ b/solution.py
@@ -355,11 +355,11 @@
 
     pl.semaphore_signal(barrier, inc=1, device_id={"grp": 1 - g}, device_id_type=MESH)
 
-    normed = normalize_rows(hidden_ref[...].astype(f32), row_of(attn_gain)).astype(bf16)
-    moved = ordered(stack_lanes(normed), order_ref)
-    for k in range(model // LANES):
-        normed_v[:, k * LANES : (k + 1) * LANES] = moved[k * rows : (k + 1) * rows]
-    pl.semaphore_wait(barrier, count_t * count_s)
+    with jax.named_scope("norm"):
+        normed = normalize_rows(hidden_ref[...].astype(f32), row_of(attn_gain)).astype(bf16)
+        moved = ordered(stack_lanes(normed), order_ref)
+        for k in range(model // LANES):
+            normed_v[:, k * LANES : (k + 1) * LANES] = moved[k * rows : (k + 1) * rows]
 
     swaps = [
         pltpu.make_async_remote_copy(
@@ -388,10 +388,12 @@
         )
         return carry
 
-    lax.fori_loop(0, steps, qkv_step, 0)
-    for copy in swaps + loads:
-        copy.start()
-    qkv_send[...] = (qkv_acc[...] * row_of(qkv_scale)).astype(bf16)
+    with jax.named_scope("qkv"):
+        lax.fori_loop(0, steps, qkv_step, 0)
+        pl.semaphore_wait(barrier, count_t * count_s)
+        for copy in swaps + loads:
+            copy.start()
+        qkv_send[...] = (qkv_acc[...] * row_of(qkv_scale)).astype(bf16)
 
     def peer_of(shift):
         return lax.rem(t + shift, count_t)
@@ -419,7 +421,8 @@
         out_u[:, part] = unpack_slab(out_w[:, part])
         return carry
 
-    lax.fori_loop(0, out_steps, unpack_out, 0)
+    with jax.named_scope("unpack_out"):
+        lax.fori_loop(0, out_steps, unpack_out, 0)
 
     row_index = lax.broadcasted_iota(jnp.int32, (mine, HEAD_SIZE), 0)
     lane = lax.broadcasted_iota(jnp.int32, (mine, HEAD_SIZE), 1)
@@ -434,8 +437,9 @@
     sine = jnp.sin(angle)
     sine = jnp.where(low, -sine, sine)
 
-    for shift in range(1, count_t):
-        qkv_copy(t, peer_of(shift)).wait_recv()
+    with jax.named_scope("wait_qkv"):
+        for shift in range(1, count_t):
+            qkv_copy(t, peer_of(shift)).wait_recv()
 
     per_share = qkv_columns // HEAD_SIZE
 
@@ -443,75 +447,83 @@
         column = (h % per_share) * HEAD_SIZE
         return qkv_recv[h // per_share, :, column : column + HEAD_SIZE]
 
-    def turned(h, gain):
-        value = normalize_rows(head_of(h).astype(f32), gain)
+    def turned(first, count, gain):
+        stacked = jnp.concatenate([head_of(first + k) for k in range(count)], axis=0)
+        value = normalize_rows(stacked.astype(f32), gain)
         other = pltpu.roll(value, half_dim, 1)
-        return (value * cosine + other * sine).astype(bf16).astype(f32)
+        wide = [jnp.concatenate([table] * count, axis=0) for table in (cosine, sine)]
+        return (value * wide[0] + other * wide[1]).astype(bf16).astype(f32)
 
     logit_scale = 1.0 / math.sqrt(HEAD_SIZE)
     q_row, k_row = row_of(q_gain), row_of(k_gain)
-    for kv in range(KEY_VALUE_HEADS):
-        new_key = turned(heads + kv, k_row)
-        for h in range(kv * per_kv, (kv + 1) * per_kv):
-            query = turned(h, q_row)
-            q_v[h * mine : (h + 1) * mine] = query
+    with jax.named_scope("rope"):
+        new_keys = turned(heads, KEY_VALUE_HEADS, k_row)
+        for kv in range(KEY_VALUE_HEADS):
+            part = slice(kv * per_kv * mine, (kv + 1) * per_kv * mine)
+            query = turned(kv * per_kv, per_kv, q_row)
+            q_v[part] = query
+            new_key = jnp.concatenate([new_keys[kv * mine : (kv + 1) * mine]] * per_kv, axis=0)
             own = jnp.sum(query * new_key, axis=1, keepdims=True) * logit_scale
-            own_v[h * mine : (h + 1) * mine] = jnp.broadcast_to(own, (mine, HEAD_SIZE))
+            own_v[part] = jnp.broadcast_to(own, query.shape)
     for copy in cache:
-        copy.wait()
+            copy.wait()
 
     zeros = jnp.zeros((per_kv, HEAD_SIZE), f32)
-    for b in range(mine):
-        query = q_v[pl.ds(b, heads, stride=mine), :]
-        spread = jnp.concatenate(
-            [
-                jnp.concatenate(
-                    [
-                        query[kv * per_kv : (kv + 1) * per_kv] if kv == place_of else zeros
-                        for place_of in range(KEY_VALUE_HEADS)
-                    ],
-                    axis=1,
-                )
-                for kv in range(KEY_VALUE_HEADS)
-            ],
-            axis=0,
-        ).astype(bf16)
-        score_v[b * heads : (b + 1) * heads] = lax.dot_general(
-            spread, keys_v[b], (((1,), (1,)), ((), ())), preferred_element_type=f32
-        )
+    with jax.named_scope("scores"):
+        for b in range(mine):
+            query = q_v[pl.ds(b, heads, stride=mine), :]
+            spread = jnp.concatenate(
+                [
+                    jnp.concatenate(
+                        [
+                            query[kv * per_kv : (kv + 1) * per_kv] if kv == place_of else zeros
+                            for place_of in range(KEY_VALUE_HEADS)
+                        ],
+                        axis=1,
+                    )
+                    for kv in range(KEY_VALUE_HEADS)
+                ],
+                axis=0,
+            ).astype(bf16)
+            score_v[b * heads : (b + 1) * heads] = lax.dot_general(
+                spread, keys_v[b], (((1,), (1,)), ((), ())), preferred_element_type=f32
+            )
     position = lax.broadcasted_iota(jnp.int32, (heads, positions), 1)
-    for b in range(mine):
-        strided = pl.ds(b, heads, stride=mine)
-        scores = score_v[b * heads : (b + 1) * heads] * logit_scale
-        scores = jnp.where(position < lengths[0, b], scores, -jnp.inf)
-        own = own_v[strided, :][:, :1]
-        top = jnp.maximum(jnp.max(scores, axis=1, keepdims=True), own)
-        weight = jnp.exp(scores - top)
-        own_e = jnp.exp(own - top)
-        denominator = jnp.sum(weight, axis=1, keepdims=True) + own_e
-        score_v[b * heads : (b + 1) * heads] = weight
-        own_e_v[strided, :] = jnp.broadcast_to(own_e, (heads, HEAD_SIZE))
-        denom_v[strided, :] = jnp.broadcast_to(denominator, (heads, HEAD_SIZE))
-    for b in range(mine):
-        mixed = jnp.dot(
-            score_v[b * heads : (b + 1) * heads].astype(bf16),
-            values_v[b],
-            preferred_element_type=f32,
-        )
-        attn_v[pl.ds(b, heads, stride=mine), :] = jnp.concatenate(
-            [
-                mixed[kv * per_kv : (kv + 1) * per_kv, kv * HEAD_SIZE : (kv + 1) * HEAD_SIZE]
-                for kv in range(KEY_VALUE_HEADS)
-            ],
-            axis=0,
-        )
-    finished = []
-    for h in range(heads):
-        part = slice(h * mine, (h + 1) * mine)
-        new_value = head_of(heads + KEY_VALUE_HEADS + h // per_kv).astype(f32)
-        own_low = own_e_v[part].astype(bf16).astype(f32)
-        finished.append(((attn_v[part] + own_low * new_value) / denom_v[part]).astype(bf16))
-    attn_send[...] = ordered(jnp.concatenate(finished, axis=0), order_ref)
+    with jax.named_scope("softmax"):
+        for b in range(mine):
+            strided = pl.ds(b, heads, stride=mine)
+            scores = score_v[b * heads : (b + 1) * heads] * logit_scale
+            scores = jnp.where(position < lengths[0, b], scores, -jnp.inf)
+            own = own_v[strided, :][:, :1]
+            top = jnp.maximum(jnp.max(scores, axis=1, keepdims=True), own)
+            weight = jnp.exp(scores - top)
+            own_e = jnp.exp(own - top)
+            denominator = jnp.sum(weight, axis=1, keepdims=True) + own_e
+            score_v[b * heads : (b + 1) * heads] = weight
+            own_e_v[strided, :] = jnp.broadcast_to(own_e, (heads, HEAD_SIZE))
+            denom_v[strided, :] = jnp.broadcast_to(denominator, (heads, HEAD_SIZE))
+    with jax.named_scope("mix"):
+        for b in range(mine):
+            mixed = jnp.dot(
+                score_v[b * heads : (b + 1) * heads].astype(bf16),
+                values_v[b],
+                preferred_element_type=f32,
+            )
+            attn_v[pl.ds(b, heads, stride=mine), :] = jnp.concatenate(
+                [
+                    mixed[kv * per_kv : (kv + 1) * per_kv, kv * HEAD_SIZE : (kv + 1) * HEAD_SIZE]
+                    for kv in range(KEY_VALUE_HEADS)
+                ],
+                axis=0,
+            )
+    with jax.named_scope("finish_attn"):
+        finished = []
+        for h in range(heads):
+            part = slice(h * mine, (h + 1) * mine)
+            new_value = head_of(heads + KEY_VALUE_HEADS + h // per_kv).astype(f32)
+            own_low = own_e_v[part].astype(bf16).astype(f32)
+            finished.append(((attn_v[part] + own_low * new_value) / denom_v[part]).astype(bf16))
+        attn_send[...] = ordered(jnp.concatenate(finished, axis=0), order_ref)
 
     head_rows = heads_t * mine
 
@@ -528,16 +540,27 @@
     for shift in range(1, count_t):
         attn_copy(peer_of(shift), t).start()
     attn_recv[t] = attn_send[pl.ds(pl.multiple_of(t * head_rows, head_rows), head_rows), :]
-    for shift in range(1, count_t):
-        attn_copy(t, peer_of(shift)).wait_recv()
+    with jax.named_scope("wait_attn"):
+        for shift in range(1, count_t):
+            attn_copy(t, peer_of(shift)).wait_recv()
 
     def proj_copy(peer, slot, i):
         part = pl.ds(pl.multiple_of(i * out_width, LANES), out_width)
         return pltpu.make_async_remote_copy(
             src_ref=proj_v.at[rows_of(peer), part],
             dst_ref=proj_recv.at[slot, :, part],
-            send_sem=proj_send_sem.at[peer, i],
-            recv_sem=proj_recv_sem.at[slot, i],
+            send_sem=proj_send_sem.at[peer],
+            recv_sem=proj_recv_sem.at[slot],
+            device_id={"tp": peer},
+            device_id_type=MESH,
+        )
+
+    def proj_whole(peer, slot):
+        return pltpu.make_async_remote_copy(
+            src_ref=proj_v.at[rows_of(peer), :],
+            dst_ref=proj_recv.at[slot],
+            send_sem=proj_send_sem.at[peer],
+            recv_sem=proj_recv_sem.at[slot],
             device_id={"tp": peer},
             device_id_type=MESH,
         )
@@ -559,32 +582,31 @@
             proj_copy(peer_of(shift), t, i).start()
         return carry
 
-    lax.fori_loop(0, out_steps, out_step, 0)
-
-    total = hidden_ref[rows_of(t), :].astype(f32) + proj_v[rows_of(t), :].astype(f32)
-    for shift in range(1, count_t):
-        slot = peer_of(shift)
-
-        def wait_part(i, carry):
-            proj_copy(t, slot, i).wait_recv()
-            return carry
-
-        lax.fori_loop(0, out_steps, wait_part, 0)
-        total += proj_recv[slot].astype(f32)
-    mid = total.astype(bf16)
-    for tt in range(count_t):
-        mid_send[tt] = mid[:, tt * share : (tt + 1) * share]
-    moved = ordered(
-        stack_lanes(normalize_rows(mid.astype(f32), row_of(mlp_gain)).astype(bf16)), order_ref
-    )
+    with jax.named_scope("proj"):
+        lax.fori_loop(0, out_steps, out_step, 0)
+
+    with jax.named_scope("mid"):
+        total = hidden_ref[rows_of(t), :].astype(f32) + proj_v[rows_of(t), :].astype(f32)
+        for shift in range(1, count_t):
+            slot = peer_of(shift)
+
+            proj_whole(t, slot).wait_recv()
+            total += proj_recv[slot].astype(f32)
+        mid = total.astype(bf16)
+        for tt in range(count_t):
+            mid_send[tt] = mid[:, tt * share : (tt + 1) * share]
+        moved = ordered(
+            stack_lanes(normalize_rows(mid.astype(f32), row_of(mlp_gain)).astype(bf16)), order_ref
+        )
     block = model // (count_g * count_s) // LANES
-    for number in range(count_g * count_s):
-        owner = number % count_s
-        first = jnp.where(number // count_s == g, 0, block)
-        for k in range(block):
-            column = pl.multiple_of((first + k) * LANES, LANES)
-            source = number * block + k
-            x_send[owner, :, pl.ds(column, LANES)] = moved[source * mine : (source + 1) * mine]
+    with jax.named_scope("order_x"):
+        for number in range(count_g * count_s):
+            owner = number % count_s
+            first = jnp.where(number // count_s == g, 0, block)
+            for k in range(block):
+                column = pl.multiple_of((first + k) * LANES, LANES)
+                source = number * block + k
+                x_send[owner, :, pl.ds(column, LANES)] = moved[source * mine : (source + 1) * mine]
 
     def x_rows(ss, tt):
         return pl.ds(pl.multiple_of((ss * count_t + tt) * mine, mine), mine)
@@ -603,7 +625,7 @@
         return pltpu.make_async_remote_copy(
             src_ref=x_v.at[x_rows(ss, tt), :],
             dst_ref=x_v.at[x_rows(ss, tt), :],
-            send_sem=x_send_sem.at[ss, peer],
+            send_sem=x_send_sem.at[peer],
             recv_sem=x_recv_sem.at[ss, tt],
             device_id={"tp": peer},
             device_id_type=MESH,
@@ -613,7 +635,17 @@
         return pltpu.make_async_remote_copy(
             src_ref=x_send.at[s],
             dst_ref=x_v.at[x_rows(s, t), :],
-            send_sem=x_send_sem.at[s, peer],
+            send_sem=x_send_sem.at[peer],
+            recv_sem=x_recv_sem.at[s, t],
+            device_id={"tp": peer},
+            device_id_type=MESH,
+        )
+
+    def x_whole(peer):
+        return pltpu.make_async_remote_copy(
+            src_ref=x_send,
+            dst_ref=x_send,
+            send_sem=x_send_sem.at[peer],
             recv_sem=x_recv_sem.at[s, t],
             device_id={"tp": peer},
             device_id_type=MESH,
@@ -629,22 +661,34 @@
             device_id_type=MESH,
         )
 
-    for shift in range(1, count_s):
-        z_copy(lax.rem(s + shift, count_s), s).start()
-    for shift in range(1, count_t):
-        own_copy(peer_of(shift)).start()
-    x_v[x_rows(s, t), :] = x_send[s]
-    for shift in range(1, count_s):
-        ss = lax.rem(s + shift, count_s)
-        z_copy(s, ss).wait_recv()
-        for turn in range(1, count_t):
-            x_copy(peer_of(turn), ss, t).start()
+    with jax.named_scope("spread_z"):
+        def near(distance, action):
+            for other in (s + distance, s - distance):
+
+                @pl.when((other >= 0) & (other < count_s))
+                def _():
+                    action(other)
+
+        for distance in range(count_s - 1, 0, -1):
+            near(distance, lambda other: z_copy(other, s).start())
+        for shift in range(1, count_t):
+            own_copy(peer_of(shift)).start()
+        x_v[x_rows(s, t), :] = x_send[s]
+
+        def forward(ss):
+            z_copy(s, ss).wait_recv()
+            for turn in range(1, count_t):
+                x_copy(peer_of(turn), ss, t).start()
+
+        for distance in range(1, count_s):
+            near(distance, forward)
     for shift in range(1, count_t):
         mid_copy(peer_of(shift), t).start()
     mid_v[rows_of(t), :] = mid_send[t]
-    for ss in range(count_s):
-        for turn in range(1, count_t):
-            x_copy(t, ss, peer_of(turn)).wait_recv()
+    with jax.named_scope("spread_t"):
+        for ss in range(count_s):
+            for turn in range(1, count_t):
+                x_copy(t, ss, peer_of(turn)).wait_recv()
 
     def finish():
         for shift in range(1, count_t):
@@ -653,13 +697,8 @@
             attn_copy(peer, t).wait_send()
             mid_copy(peer, t).wait_send()
 
-            def wait_part(i, carry):
-                proj_copy(peer, t, i).wait_send()
-                return carry
-
-            lax.fori_loop(0, out_steps, wait_part, 0)
-            for ss in range(count_s):
-                x_copy(peer, ss, t).wait_send()
+            proj_whole(peer, t).wait_send()
+            x_whole(peer).wait_send()
         for shift in range(1, count_s):
             z_copy(lax.rem(s + shift, count_s), s).wait_send()
         for copy in swaps:
@@ -672,9 +711,10 @@
     return swaps, loads, mid_wait, finish
 
 
-def mlp_phase(here, lag, scales, mlp_buffers, scratch, sems, attention, out_ref):
+def mlp_phase(here, lags, scales, mlp_buffers, scratch, sems, attention, out_ref):
     g, t, s, count_g, count_t, count_s = here
     gate_scale, up_scale, down_scale, order_ref = scales
+    lag, back_lag = lags
     gate_v, up_v, down_v, x_v, mid_v = mlp_buffers
     partial, sum_recv, act, total, part_send, part_recv = scratch
     (
@@ -695,14 +735,14 @@
     total[...] = jnp.zeros_like(total)
 
     last = count_s - 1
-    far = last * lag
+    far = (last - 1) * lag
     toward = (s - 1, s + 1)
 
     def sum_copy(side, j):
         return pltpu.make_async_remote_copy(
-            src_ref=partial.at[j, side],
+            src_ref=partial.at[side, j],
             dst_ref=sum_recv.at[side, j],
-            send_sem=sum_send_sem.at[side, j],
+            send_sem=sum_send_sem.at[side],
             recv_sem=sum_recv_sem.at[side, j],
             device_id={"src": toward[side]},
             device_id_type=MESH,
@@ -710,47 +750,50 @@
 
     def act_copy(side, j):
         return pltpu.make_async_remote_copy(
-            src_ref=act.at[j, side],
-            dst_ref=act.at[j, side],
-            send_sem=act_send_sem.at[side, j],
+            src_ref=act.at[side, j],
+            dst_ref=act.at[side, j],
+            send_sem=act_send_sem.at[side],
             recv_sem=act_recv_sem.at[side, j],
             device_id={"src": toward[1 - side]},
             device_id_type=MESH,
         )
 
+    def whole_copy(array, side, sem):
+        return pltpu.make_async_remote_copy(
+            src_ref=array.at[side],
+            dst_ref=array.at[side],
+            send_sem=sem.at[side],
+            recv_sem=sum_recv_sem.at[side, 0],
+            device_id={"src": toward[side]},
+            device_id_type=MESH,
+        )
+
     def depth_of(side):
         return last - s if side == 0 else s
 
-    def sum_step(side, j):
+    def pass_step(side, j):
         depth = depth_of(side)
-        at_end = depth == last
 
         @pl.when(depth > 0)
         def _():
             sum_copy(side, j).wait_recv()
-
-        @pl.when(depth == 0)
-        def _():
-            sum_copy(side, j).start()
-
-        @pl.when((depth > 0) & jnp.logical_not(at_end))
-        def _():
-            partial[j, side] = (
-                partial[j, side].astype(jnp.float32) + sum_recv[side, j].astype(jnp.float32)
+            partial[side, j] = (
+                partial[side, j].astype(jnp.float32) + sum_recv[side, j].astype(jnp.float32)
             ).astype(jnp.bfloat16)
-            sum_copy(side, j).start()
-
-        @pl.when(at_end)
-        def _():
-            value = partial[j, side].astype(jnp.float32) + sum_recv[side, j].astype(jnp.float32)
-            columns = pl.ds(pl.multiple_of(j * LANES, LANES), LANES)
-            gate_value = value[:, :LANES] * gate_scale[columns].reshape(1, LANES)
-            up_value = value[:, LANES:] * up_scale[columns].reshape(1, LANES)
-            activated = (gate_value / (1.0 + jnp.exp(-gate_value)) * up_value).astype(jnp.bfloat16)
-            act[j, side] = jnp.dot(
-                activated, order_ref[...], preferred_element_type=jnp.float32
-            ).astype(jnp.bfloat16)
-            act_copy(side, j).start()
+
+        sum_copy(side, j).start()
+
+    def end_step(side, j):
+        sum_copy(side, j).wait_recv()
+        value = partial[side, j].astype(jnp.float32) + sum_recv[side, j].astype(jnp.float32)
+        columns = pl.ds(pl.multiple_of(j * LANES, LANES), LANES)
+        gate_value = value[:, :LANES] * gate_scale[columns].reshape(1, LANES)
+        up_value = value[:, LANES:] * up_scale[columns].reshape(1, LANES)
+        activated = (gate_value / (1.0 + jnp.exp(-gate_value)) * up_value).astype(jnp.bfloat16)
+        act[side, j] = jnp.dot(
+            activated, order_ref[...], preferred_element_type=jnp.float32
+        ).astype(jnp.bfloat16)
+        act_copy(side, j).start()
 
     def act_step(side, j):
         depth = last - depth_of(side)
@@ -777,25 +820,38 @@
             )
             product = jnp.dot(x_v[...], weights, preferred_element_type=jnp.float32)
             product = product.astype(jnp.bfloat16)
-            partial[i, 0] = product[:half]
-            partial[i, 1] = product[half:]
+            partial[0, i] = product[:half]
+            partial[1, i] = product[half:]
 
         for side in range(2):
-            j = i - depth_of(side) * lag
-
-            @pl.when((j >= 0) & (j < chunks))
+            depth = depth_of(side)
+            j = i - depth * lag
+
+            @pl.when((depth < last) & (j >= 0) & (j < chunks))
             def _():
-                sum_step(side, j)
-
+                pass_step(side, j)
+
+        return carry
+
+    def end_loop(j, carry):
+        for side in range(2):
+
+            @pl.when(depth_of(side) == last)
+            def _():
+                end_step(side, j)
+
+        return carry
+
+    def back_step(i, carry):
         for side in range(2):
             depth = last - depth_of(side)
-            j = i - far - depth * lag
+            j = i - depth * back_lag
 
             @pl.when((depth > 0) & (j >= 0) & (j < chunks))
             def _():
                 act_step(side, j)
 
-        j = i - far - jnp.maximum(s, last - s) * lag
+        j = i - jnp.maximum(s, last - s) * back_lag
 
         @pl.when((j >= 0) & (j < chunks))
         def _():
@@ -811,12 +867,17 @@
             )
             for side in range(2):
                 total[side * half : (side + 1) * half] += jnp.dot(
-                    act[j, side], weights, preferred_element_type=jnp.float32
+                    act[side, j], weights, preferred_element_type=jnp.float32
                 )
 
         return carry
 
-    lax.fori_loop(0, chunks + 2 * far, step, 0)
+    with jax.named_scope("mlp_loop"):
+        lax.fori_loop(0, chunks + far, step, 0)
+    with jax.named_scope("end_loop"):
+        lax.fori_loop(0, chunks, end_loop, 0)
+    with jax.named_scope("back_loop"):
+        lax.fori_loop(0, chunks + last * back_lag, back_step, 0)
 
     per_share = count_g * count_s // count_t
 
@@ -833,48 +894,64 @@
             device_id_type=MESH,
         )
 
-    for shift in range(count_s):
-        ss = lax.rem(s + 1 + shift, count_s)
-        row = pl.ds(pl.multiple_of(ss * group_rows, group_rows), group_rows)
-        for index in range(2):
-            owner, slot, copy = part_copy(index, ss)
-            piece = total[row, index * block : (index + 1) * block].astype(jnp.bfloat16)
-            mine = (owner == t) & (ss == s)
-
-            @pl.when(mine)
+    with jax.named_scope("part_send"):
+        for shift in range(count_s):
+            ss = send_order(s, count_s, shift)
+            row = pl.ds(pl.multiple_of(ss * group_rows, group_rows), group_rows)
+            for index in range(2):
+                owner, slot, copy = part_copy(index, ss)
+                piece = total[row, index * block : (index + 1) * block].astype(jnp.bfloat16)
+                mine = (owner == t) & (ss == s)
+
+                @pl.when(mine)
+                def _():
+                    part_recv[slot] = piece
+
+                @pl.when(jnp.logical_not(mine))
+                def _():
+                    part_send[index, ss] = piece
+                    copy.start()
+
+    with jax.named_scope("drain"):
+        finish()
+        for side in range(2):
+            depth = depth_of(side)
+
+            @pl.when(depth < last)
             def _():
-                part_recv[slot] = piece
-
-            @pl.when(jnp.logical_not(mine))
+                whole_copy(partial, side, sum_send_sem).wait_send()
+
+            @pl.when(depth > 0)
             def _():
-                part_send[index, ss] = piece
-                copy.start()
-
-    for slot in range(count_t * per_share):
-        number = t * per_share + slot % per_share
-        from_me = (slot // per_share == t) & (lax.rem(number, count_s) == s)
-
-        @pl.when(jnp.logical_not(from_me))
-        def _():
-            pltpu.make_async_remote_copy(
-                src_ref=part_send.at[0, 0],
-                dst_ref=part_recv.at[slot],
-                send_sem=part_send_sem.at[0, 0],
-                recv_sem=part_recv_sem.at[slot],
-                device_id={"tp": t, "src": s},
-                device_id_type=MESH,
-            ).wait_recv()
+                whole_copy(act, side, act_send_sem).wait_send()
+
+    with jax.named_scope("part_wait"):
+        for slot in range(count_t * per_share):
+            number = t * per_share + slot % per_share
+            from_me = (slot // per_share == t) & (lax.rem(number, count_s) == s)
+
+            @pl.when(jnp.logical_not(from_me))
+            def _():
+                pltpu.make_async_remote_copy(
+                    src_ref=part_send.at[0, 0],
+                    dst_ref=part_recv.at[slot],
+                    send_sem=part_send_sem.at[0, 0],
+                    recv_sem=part_recv_sem.at[slot],
+                    device_id={"tp": t, "src": s},
+                    device_id_type=MESH,
+                ).wait_recv()
 
     mid_wait()
-    for place in range(per_share):
-        value = part_recv[place].astype(jnp.float32)
-        for tt in range(1, count_t):
-            value += part_recv[tt * per_share + place].astype(jnp.float32)
-        columns = slice(place * block, (place + 1) * block)
-        scale_at = pl.ds(pl.multiple_of((t * per_share + place) * block, LANES), block)
-        out_ref[:, columns] = (
-            mid_v[:, columns].astype(jnp.float32) + value * down_scale[scale_at].reshape(1, block)
-        ).astype(jnp.bfloat16)
+    with jax.named_scope("part_sum"):
+        for place in range(per_share):
+            value = part_recv[place].astype(jnp.float32)
+            for tt in range(1, count_t):
+                value += part_recv[tt * per_share + place].astype(jnp.float32)
+            columns = slice(place * block, (place + 1) * block)
+            scale_at = pl.ds(pl.multiple_of((t * per_share + place) * block, LANES), block)
+            out_ref[:, columns] = (
+                mid_v[:, columns].astype(jnp.float32) + value * down_scale[scale_at].reshape(1, block)
+            )
 
     for ss in range(count_s):
         for index in range(2):
@@ -884,25 +961,17 @@
             def _():
                 copy.wait_send()
 
-    def drain(j, carry):
-        for side in range(2):
-            depth = depth_of(side)
-
-            @pl.when(depth < last)
-            def _():
-                sum_copy(side, j).wait_send()
-
-            @pl.when(depth > 0)
-            def _():
-                act_copy(side, j).wait_send()
-
-        return carry
-
-    lax.fori_loop(0, chunks, drain, 0)
-    finish()
-
-
-def layer_kernel(lag, counts, *refs):
+
+def send_order(s, count_s, shift):
+    if count_s % 2:
+        return lax.rem(s + 1 + shift, count_s)
+    size = count_s // 2
+    other = jnp.where(s < size, size, 0)
+    base = other if shift < size else size - other
+    return base + lax.rem(s + 1 + shift, size)
+
+
+def layer_kernel(lags, counts, *refs):
     count_in, count_buffers, count_a, count_asem, count_b, count_bsem = counts
     take = iter(refs)
 
@@ -928,9 +997,10 @@
         up_scale,
         w_down,
         down_scale,
-        order_ref,
     ) = some(count_in)
     out_ref = next(take)
+    order_ref = next(take)
+    order_ref[...] = lane_order(LANES)
     mlp_buffers = some(count_buffers)
     scratch_a, sems_a = some(count_a), some(count_asem)
     scratch_b, sems_b = some(count_b), some(count_bsem)
@@ -961,7 +1031,7 @@
     )
     mlp_phase(
         here,
-        lag,
+        lags,
         (gate_scale, up_scale, down_scale, order_ref),
         mlp_buffers,
         scratch_b,
@@ -971,7 +1041,7 @@
     )
 
 
-def layer(args, lag):
+def layer(args, lags):
     (
         hidden_in,
         attn_gain,
@@ -1053,31 +1123,31 @@
         dma((count_t,)),
         dma((count_t,)),
         dma((count_t,)),
-        dma((count_t, out_steps)),
-        dma((count_t, out_steps)),
+        dma((count_t,)),
+        dma((count_t,)),
         dma((count_t,)),
         dma((count_t,)),
         dma((count_s,)),
-        dma((count_s, count_t)),
+        dma((count_t,)),
         dma((count_s, count_t)),
     ]
     scratch_b = [
-        pltpu.VMEM((chunks, 2, half, 2 * LANES), bf16),
         pltpu.VMEM((2, chunks, half, 2 * LANES), bf16),
-        pltpu.VMEM((chunks, 2, half, LANES), bf16),
+        pltpu.VMEM((2, chunks, half, 2 * LANES), bf16),
+        pltpu.VMEM((2, chunks, half, LANES), bf16),
         pltpu.VMEM((rows, depth), f32),
         pltpu.VMEM((2, count_s, group_rows, block), bf16),
         pltpu.VMEM((slots, group_rows, block), bf16),
     ]
     sems_b = [
+        dma((2,)),
         dma((2, chunks)),
-        dma((2, chunks)),
-        dma((2, chunks)),
+        dma((2,)),
         dma((2, chunks)),
         dma((2, count_s)),
         dma((slots,)),
     ]
-    specs = [vmem] * (len(args) + 1)
+    specs = [vmem] * len(args)
     for place in (2, 6, 7, 9, 12, 13, 16):
         specs[place] = hbm
     specs[8] = smem
@@ -1090,16 +1160,16 @@
         len(sems_b),
     )
     return pl.pallas_call(
-        functools.partial(layer_kernel, lag, counts),
-        out_shape=jax.ShapeDtypeStruct((group_rows, share), bf16),
+        functools.partial(layer_kernel, lags, counts),
+        out_shape=jax.ShapeDtypeStruct((group_rows, share), f32),
         in_specs=specs,
         out_specs=vmem,
-        scratch_shapes=buffers + scratch_a + sems_a + scratch_b + sems_b,
+        scratch_shapes=[pltpu.VMEM((LANES, LANES), bf16)] + buffers + scratch_a + sems_a + scratch_b + sems_b,
         compiler_params=pltpu.CompilerParams(
             collective_id=1, has_side_effects=True, vmem_limit_bytes=63 * 1024 * 1024
         ),
         name="layer",
-    )(*args, lane_order(LANES))
+    )(*args).astype(bf16)
 
 
 def fast_layer(args):
@@ -1166,7 +1236,7 @@
         down_scale,
     )
     if fast_layer(args):
-        return layer(args, 2)
+        return layer(args, (4, 6))
     tp_count = lax.axis_size("tp")
     tp_index = lax.axis_index("tp")
     share_cols = D // tp_count

time: 129 us -> 116 us (0.90)
  Pallas kernels: 125 us -> 113 us
  local copies, waits for them, and re-layouts: 1.59 us -> 0 us
    pallas_call x1, Pallas kernels: 125 us -> 113 us  [layer(): pl.pallas_call(functools.partial(layer_kernel, lags, counts), out_shape=j...]
    unnamed x1 -> x0, local copies, waits for them, and re-layouts: 1.59 us -> none
where the time goes in v3:
time: 116 us; the launch traced here: 115 us
  Pallas kernels  113 us (97%)
  other arithmetic  1.66 us (1%)
    pallas_call x1, Pallas kernels, layer(): pl.pallas_call(functools.partial(layer_kernel, lags, counts), out_shape=j...  113 us

profile of v3, /device:TPU:0, one launch (start us, length us, event | category | flops | bytes accessed | tf_op | source)
XLA Modules:
  0.0 115.2 jit_solution(8121812578965366956)
XLA Ops:
  0.0 113.5 %layer.1 = f32[64,1280]{1,0:T(8,128)} custom-call(bf16[64,5120]{1,0:T(8,128)(2,1)} %refs_0_.1, f32[5120]{0:T(1024)} %refs_1_.1, s32[1280,1280]{1,0:T(8,128)} %refs_2_.1, f32[1280]{0:T(1024)} %refs_3_.1, f32[128]{0:T(128)} %refs_4_.1, f32[128]{0:T(128)} %refs_5_.1, bf16[1,16,128,512]{3,2,1,0:T(8,128)(2,1)} %refs_6_.1, bf16[1,16,128,512]{3,2,1,0:T(8,128)(2,1)} %refs_7_.1, ...), custom_call_target="tpu_custom_call" | custom-call | tf_op jit(solution)/shard_map/layer/pallas_call | solution.py:1162
  113.5 1.7 %convert_element_type.3 = bf16[64,1280]{1,0:T(8,128)(2,1)} convert(f32[64,1280]{1,0:T(8,128)} %layer.1) | non-fusion elementwise | flops 81920 | bytes 491520 | tf_op jit(solution)/shard_map/convert_element_type | solution.py:1172

commit v4 on v3

--- a/solution.py
+++ b/solution.py
@@ -232,7 +232,7 @@
     for k in range(rows // slab):
         words = packed[k * slab : (k + 1) * slab]
         for j in range(4):
-            parts.append(unpack_bytes(words, j).astype(jnp.float32).astype(jnp.bfloat16))
+            parts.append(jnp.right_shift(words, 8 * j).astype(jnp.int8).astype(jnp.bfloat16))
     return jnp.concatenate(parts, axis=0)
 
 
@@ -494,14 +494,14 @@
             strided = pl.ds(b, heads, stride=mine)
             scores = score_v[b * heads : (b + 1) * heads] * logit_scale
             scores = jnp.where(position < lengths[0, b], scores, -jnp.inf)
-            own = own_v[strided, :][:, :1]
+            own = own_v[strided, :]
             top = jnp.maximum(jnp.max(scores, axis=1, keepdims=True), own)
             weight = jnp.exp(scores - top)
             own_e = jnp.exp(own - top)
             denominator = jnp.sum(weight, axis=1, keepdims=True) + own_e
             score_v[b * heads : (b + 1) * heads] = weight
-            own_e_v[strided, :] = jnp.broadcast_to(own_e, (heads, HEAD_SIZE))
-            denom_v[strided, :] = jnp.broadcast_to(denominator, (heads, HEAD_SIZE))
+            own_e_v[strided, :] = own_e
+            denom_v[strided, :] = denominator
     with jax.named_scope("mix"):
         for b in range(mine):
             mixed = jnp.dot(
@@ -685,10 +685,13 @@
     for shift in range(1, count_t):
         mid_copy(peer_of(shift), t).start()
     mid_v[rows_of(t), :] = mid_send[t]
-    with jax.named_scope("spread_t"):
-        for ss in range(count_s):
+    def x_wait(side):
+        groups = count_s // 2
+        base = jnp.where(side == 1, 0, groups)
+        for k in range(groups):
             for turn in range(1, count_t):
-                x_copy(t, ss, peer_of(turn)).wait_recv()
+                x_copy(t, base + k, peer_of(turn)).wait_recv()
+
 
     def finish():
         for shift in range(1, count_t):
@@ -708,13 +711,13 @@
         for shift in range(1, count_t):
             mid_copy(t, peer_of(shift)).wait_recv()
 
-    return swaps, loads, mid_wait, finish
+    return swaps, loads, mid_wait, x_wait, finish
 
 
 def mlp_phase(here, lags, scales, mlp_buffers, scratch, sems, attention, out_ref):
     g, t, s, count_g, count_t, count_s = here
     gate_scale, up_scale, down_scale, order_ref = scales
-    lag, back_lag = lags
+    lag, back_lag, far_lag, back_start = lags
     gate_v, up_v, down_v, x_v, mid_v = mlp_buffers
     partial, sum_recv, act, total, part_send, part_recv = scratch
     (
@@ -725,7 +728,7 @@
         part_send_sem,
         part_recv_sem,
     ) = sems
-    swaps, loads, mid_wait, finish = attention
+    swaps, loads, mid_wait, x_wait, finish = attention
     rows = x_v.shape[0]
     half = rows // 2
     hidden = gate_v.shape[2]
@@ -736,7 +739,9 @@
 
     last = count_s - 1
     far = (last - 1) * lag
-    toward = (s - 1, s + 1)
+
+    def toward(side):
+        return s - 1 + 2 * side
 
     def sum_copy(side, j):
         return pltpu.make_async_remote_copy(
@@ -744,7 +749,7 @@
             dst_ref=sum_recv.at[side, j],
             send_sem=sum_send_sem.at[side],
             recv_sem=sum_recv_sem.at[side, j],
-            device_id={"src": toward[side]},
+            device_id={"src": toward(side)},
             device_id_type=MESH,
         )
 
@@ -754,7 +759,7 @@
             dst_ref=act.at[side, j],
             send_sem=act_send_sem.at[side],
             recv_sem=act_recv_sem.at[side, j],
-            device_id={"src": toward[1 - side]},
+            device_id={"src": toward(1 - side)},
             device_id_type=MESH,
         )
 
@@ -764,12 +769,14 @@
             dst_ref=array.at[side],
             send_sem=sem.at[side],
             recv_sem=sum_recv_sem.at[side, 0],
-            device_id={"src": toward[side]},
+            device_id={"src": toward(side)},
             device_id_type=MESH,
         )
 
     def depth_of(side):
-        return last - s if side == 0 else s
+        if isinstance(side, int):
+            return last - s if side == 0 else s
+        return jnp.where(side == 0, last - s, s)
 
     def pass_step(side, j):
         depth = depth_of(side)
@@ -803,27 +810,33 @@
         def _():
             act_copy(side, j).start()
 
+    near = jnp.where(2 * s < count_s, 1, 0)
+    is_end = (s == 0) | (s == last)
+
+    def product_step(side, i):
+        columns = pl.ds(pl.multiple_of(i * LANES, LANES), LANES)
+        gate_w = [unpack_slab(gate_v[index, :, columns]) for index in range(2)]
+        up_w = [unpack_slab(up_v[index, :, columns]) for index in range(2)]
+        weights = jnp.concatenate(
+            [jnp.concatenate(gate_w, axis=0), jnp.concatenate(up_w, axis=0)], axis=1
+        )
+        row = pl.ds(pl.multiple_of((1 - side) * half, half), half)
+        partial[side, i] = jnp.dot(
+            x_v[row, :], weights, preferred_element_type=jnp.float32
+        ).astype(jnp.bfloat16)
+
     def step(i, carry):
-        @pl.when(i < chunks)
-        def _():
-            @pl.when(i == 0)
+        for side, wait in ((near, 0), (1 - near, far_lag)):
+            k = i - wait
+
+            @pl.when((k >= 0) & (k < chunks))
             def _():
-                for index in range(2):
-                    loads[index].wait()
-                    swaps[index].wait_recv()
-
-            columns = pl.ds(pl.multiple_of(i * LANES, LANES), LANES)
-            gate_w = [unpack_slab(gate_v[index, :, columns]) for index in range(2)]
-            up_w = [unpack_slab(up_v[index, :, columns]) for index in range(2)]
-            weights = jnp.concatenate(
-                [jnp.concatenate(gate_w, axis=0), jnp.concatenate(up_w, axis=0)], axis=1
-            )
-            product = jnp.dot(x_v[...], weights, preferred_element_type=jnp.float32)
-            product = product.astype(jnp.bfloat16)
-            partial[0, i] = product[:half]
-            partial[1, i] = product[half:]
-
-        for side in range(2):
+                @pl.when(k == 0)
+                def _():
+                    x_wait(side)
+
+                product_step(side, k)
+
             depth = depth_of(side)
             j = i - depth * lag
 
@@ -866,12 +879,15 @@
                 [unpack_slab(down_v[index, words, :]) for index in range(2)], axis=1
             )
             for side in range(2):
-                total[side * half : (side + 1) * half] += jnp.dot(
+                total[(1 - side) * half : (2 - side) * half] += jnp.dot(
                     act[side, j], weights, preferred_element_type=jnp.float32
                 )
 
         return carry
 
+    for index in range(2):
+        loads[index].wait()
+        swaps[index].wait_recv()
     with jax.named_scope("mlp_loop"):
         lax.fori_loop(0, chunks + far, step, 0)
     with jax.named_scope("end_loop"):
@@ -1161,7 +1177,7 @@
     )
     return pl.pallas_call(
         functools.partial(layer_kernel, lags, counts),
-        out_shape=jax.ShapeDtypeStruct((group_rows, share), f32),
+        out_shape=pltpu.VMEM((group_rows, share), f32),
         in_specs=specs,
         out_specs=vmem,
         scratch_shapes=[pltpu.VMEM((LANES, LANES), bf16)] + buffers + scratch_a + sems_a + scratch_b + sems_b,
@@ -1236,7 +1252,7 @@
         down_scale,
     )
     if fast_layer(args):
-        return layer(args, (4, 6))
+        return layer(args, (4, 6, 4, 4))
     tp_count = lax.axis_size("tp")
     tp_index = lax.axis_index("tp")
     share_cols = D // tp_count

time: 116 us -> 111 us (0.957)
  Pallas kernels: 113 us -> 109 us
    pallas_call x1, Pallas kernels: 113 us -> 109 us  [layer(): pl.pallas_call(functools.partial(layer_kernel, lags, counts), out_shape=p...]
where the time goes in v4:
time: 111 us; the launch traced here: 110 us
  Pallas kernels  109 us (98%)
    pallas_call x1, Pallas kernels, layer(): pl.pallas_call(functools.partial(layer_kernel, lags, counts), out_shape=p...  109 us

profile of v4, /device:TPU:0, one launch (start us, length us, event | category | flops | bytes accessed | tf_op | source)
XLA Modules:
  0.0 109.9 jit_solution(10718922045214077672)
XLA Ops:
  0.0 109.2 %layer.1 = f32[64,1280]{1,0:T(8,128)S(1)} custom-call(bf16[64,5120]{1,0:T(8,128)(2,1)} %refs_0_.1, f32[5120]{0:T(1024)} %refs_1_.1, s32[1280,1280]{1,0:T(8,128)} %refs_2_.1, f32[1280]{0:T(1024)} %refs_3_.1, f32[128]{0:T(128)} %refs_4_.1, f32[128]{0:T(128)} %refs_5_.1, bf16[1,16,128,512]{3,2,1,0:T(8,128)(2,1)} %refs_6_.1, bf16[1,16,128,512]{3,2,1,0:T(8,128)(2,1)} %refs_7_.1, ...), custom_call_target="tpu_custom_call" | custom-call | tf_op jit(solution)/shard_map/layer/pallas_call | solution.py:1178
  109.2 0.7 convert_element_type.3

commit v5 on v4

--- a/solution.py
+++ b/solution.py
@@ -717,9 +717,20 @@
 def mlp_phase(here, lags, scales, mlp_buffers, scratch, sems, attention, out_ref):
     g, t, s, count_g, count_t, count_s = here
     gate_scale, up_scale, down_scale, order_ref = scales
-    lag, back_lag, far_lag, back_start = lags
+    lag, back_lag, far_lag = lags
     gate_v, up_v, down_v, x_v, mid_v = mlp_buffers
-    partial, sum_recv, act, total, part_send, part_recv = scratch
+    (
+        partial,
+        sum_recv,
+        act,
+        total,
+        part_send,
+        part_recv,
+        stage_send,
+        stage_recv,
+        last_send,
+        last_recv,
+    ) = scratch
     (
         sum_send_sem,
         sum_recv_sem,
@@ -727,6 +738,10 @@
         act_recv_sem,
         part_send_sem,
         part_recv_sem,
+        stage_send_sem,
+        stage_recv_sem,
+        last_send_sem,
+        last_recv_sem,
     ) = sems
     swaps, loads, mid_wait, x_wait, finish = attention
     rows = x_v.shape[0]
@@ -910,72 +925,167 @@
             device_id_type=MESH,
         )
 
-    with jax.named_scope("part_send"):
+    def drain():
+        with jax.named_scope("drain"):
+            finish()
+            for side in range(2):
+                depth = depth_of(side)
+
+                @pl.when(depth < last)
+                def _():
+                    whole_copy(partial, side, sum_send_sem).wait_send()
+
+                @pl.when(depth > 0)
+                def _():
+                    whole_copy(act, side, act_send_sem).wait_send()
+
+    @pl.when(g == 0)
+    def _():
+        with jax.named_scope("part_send"):
+            for shift in range(count_s):
+                ss = send_order(s, count_s, shift)
+                row = pl.ds(pl.multiple_of(ss * group_rows, group_rows), group_rows)
+                for index in range(2):
+                    owner, slot, copy = part_copy(index, ss)
+                    piece = total[row, index * block : (index + 1) * block].astype(jnp.bfloat16)
+                    mine = (owner == t) & (ss == s)
+
+                    @pl.when(mine)
+                    def _():
+                        part_recv[slot] = piece
+
+                    @pl.when(jnp.logical_not(mine))
+                    def _():
+                        part_send[index, ss] = piece
+                        copy.start()
+
+        drain()
+        with jax.named_scope("part_wait"):
+            for slot in range(count_t * per_share):
+                number = t * per_share + slot % per_share
+                from_me = (slot // per_share == t) & (lax.rem(number, count_s) == s)
+
+                @pl.when(jnp.logical_not(from_me))
+                def _():
+                    pltpu.make_async_remote_copy(
+                        src_ref=part_send.at[0, 0],
+                        dst_ref=part_recv.at[slot],
+                        send_sem=part_send_sem.at[0, 0],
+                        recv_sem=part_recv_sem.at[slot],
+                        device_id={"tp": t, "src": s},
+                        device_id_type=MESH,
+                    ).wait_recv()
+
+        mid_wait()
+        with jax.named_scope("part_sum"):
+            for place in range(per_share):
+                value = part_recv[place].astype(jnp.float32)
+                for tt in range(1, count_t):
+                    value += part_recv[tt * per_share + place].astype(jnp.float32)
+                columns = slice(place * block, (place + 1) * block)
+                scale_at = pl.ds(pl.multiple_of((t * per_share + place) * block, LANES), block)
+                out_ref[:, columns] = (
+                    mid_v[:, columns].astype(jnp.float32) + value * down_scale[scale_at].reshape(1, block)
+                )
+
+        for ss in range(count_s):
+            for index in range(2):
+                owner, slot, copy = part_copy(index, ss)
+
+                @pl.when((owner != t) | (ss != s))
+                def _():
+                    copy.wait_send()
+
+    quarter = group_rows // count_t
+
+    def stage_copy(peer, slot):
+        return pltpu.make_async_remote_copy(
+            src_ref=stage_send.at[peer],
+            dst_ref=stage_recv.at[slot],
+            send_sem=stage_send_sem.at[peer],
+            recv_sem=stage_recv_sem.at[slot],
+            device_id={"tp": peer},
+            device_id_type=MESH,
+        )
+
+    def last_copy(index, ss, place, slot, owner):
+        return pltpu.make_async_remote_copy(
+            src_ref=last_send.at[index, ss],
+            dst_ref=last_recv.at[place, slot],
+            send_sem=last_send_sem.at[index, ss],
+            recv_sem=last_recv_sem.at[place, slot],
+            device_id={"tp": owner, "src": ss},
+            device_id_type=MESH,
+        )
+
+    def quarter_rows(ss, tt):
+        start = ss * group_rows + tt * quarter
+        return pl.ds(pl.multiple_of(start, quarter), quarter)
+
+    def target_of(index):
+        number = jnp.where(index == 0, g, count_g - 1 - g) * count_s + s
+        return number // per_share, lax.rem(number, per_share)
+
+    @pl.when(g != 0)
+    def _():
+        with jax.named_scope("stage_send"):
+            for shift in range(1, count_t):
+                peer = lax.rem(t + shift, count_t)
+                for ss in range(count_s):
+                    stage_send[peer, ss] = total[quarter_rows(ss, peer), :].astype(jnp.bfloat16)
+                stage_copy(peer, t).start()
+        drain()
+        with jax.named_scope("stage_wait"):
+            for shift in range(1, count_t):
+                stage_copy(t, lax.rem(t + shift, count_t)).wait_recv()
         for shift in range(count_s):
             ss = send_order(s, count_s, shift)
-            row = pl.ds(pl.multiple_of(ss * group_rows, group_rows), group_rows)
+            value = total[quarter_rows(ss, t), :]
+            for turn in range(1, count_t):
+                value += stage_recv[lax.rem(t + turn, count_t), ss].astype(jnp.float32)
             for index in range(2):
-                owner, slot, copy = part_copy(index, ss)
-                piece = total[row, index * block : (index + 1) * block].astype(jnp.bfloat16)
+                owner, place = target_of(index)
+                piece = value[:, index * block : (index + 1) * block].astype(jnp.bfloat16)
                 mine = (owner == t) & (ss == s)
 
                 @pl.when(mine)
                 def _():
-                    part_recv[slot] = piece
+                    last_recv[place, t] = piece
 
                 @pl.when(jnp.logical_not(mine))
                 def _():
-                    part_send[index, ss] = piece
-                    copy.start()
-
-    with jax.named_scope("drain"):
-        finish()
-        for side in range(2):
-            depth = depth_of(side)
-
-            @pl.when(depth < last)
-            def _():
-                whole_copy(partial, side, sum_send_sem).wait_send()
-
-            @pl.when(depth > 0)
-            def _():
-                whole_copy(act, side, act_send_sem).wait_send()
-
-    with jax.named_scope("part_wait"):
-        for slot in range(count_t * per_share):
-            number = t * per_share + slot % per_share
-            from_me = (slot // per_share == t) & (lax.rem(number, count_s) == s)
-
-            @pl.when(jnp.logical_not(from_me))
-            def _():
-                pltpu.make_async_remote_copy(
-                    src_ref=part_send.at[0, 0],
-                    dst_ref=part_recv.at[slot],
-                    send_sem=part_send_sem.at[0, 0],
-                    recv_sem=part_recv_sem.at[slot],
-                    device_id={"tp": t, "src": s},
-                    device_id_type=MESH,
-                ).wait_recv()
-
-    mid_wait()
-    with jax.named_scope("part_sum"):
+                    last_send[index, ss] = piece
+                    last_copy(index, ss, place, t, owner).start()
+
+        with jax.named_scope("part_wait"):
+            for place in range(per_share):
+                number = t * per_share + place
+                for tt in range(count_t):
+
+                    @pl.when((tt != t) | (lax.rem(number, count_s) != s))
+                    def _():
+                        last_copy(0, 0, place, tt, t).wait_recv()
+
+        mid_wait()
         for place in range(per_share):
-            value = part_recv[place].astype(jnp.float32)
-            for tt in range(1, count_t):
-                value += part_recv[tt * per_share + place].astype(jnp.float32)
             columns = slice(place * block, (place + 1) * block)
             scale_at = pl.ds(pl.multiple_of((t * per_share + place) * block, LANES), block)
-            out_ref[:, columns] = (
-                mid_v[:, columns].astype(jnp.float32) + value * down_scale[scale_at].reshape(1, block)
-            )
-
-    for ss in range(count_s):
-        for index in range(2):
-            owner, slot, copy = part_copy(index, ss)
-
-            @pl.when((owner != t) | (ss != s))
-            def _():
-                copy.wait_send()
+            scale = down_scale[scale_at].reshape(1, block)
+            for tt in range(count_t):
+                row = slice(tt * quarter, (tt + 1) * quarter)
+                out_ref[row, columns] = (
+                    mid_v[row, columns].astype(jnp.float32)
+                    + last_recv[place, tt].astype(jnp.float32) * scale
+                )
+        for shift in range(1, count_t):
+            stage_copy(lax.rem(t + shift, count_t), t).wait_send()
+        for ss in range(count_s):
+            for index in range(2):
+                owner, place = target_of(index)
+
+                @pl.when((owner != t) | (ss != s))
+                def _():
+                    last_copy(index, ss, place, t, owner).wait_send()
 
 
 def send_order(s, count_s, shift):
@@ -1090,7 +1200,7 @@
     share = model // count_t
     slots = count_g * count_s
     steps = 10 if w_qkv.shape[0] % 320 == 0 else w_qkv.shape[0] // 32
-    out_steps = 10 if model % (10 * LANES) == 0 else model // LANES
+    out_steps = 5 if model % (5 * LANES) == 0 else model // LANES
     qkv_columns = w_qkv.shape[1]
     head_rows = QUERY_HEADS * mine
     bf16, f32, i32 = jnp.bfloat16, jnp.float32, jnp.int32
@@ -1154,6 +1264,10 @@
         pltpu.VMEM((rows, depth), f32),
         pltpu.VMEM((2, count_s, group_rows, block), bf16),
         pltpu.VMEM((slots, group_rows, block), bf16),
+        pltpu.VMEM((count_t, count_s, mine, depth), bf16),
+        pltpu.VMEM((count_t, count_s, mine, depth), bf16),
+        pltpu.VMEM((2, count_s, mine, block), bf16),
+        pltpu.VMEM((slots // count_t, count_t, mine, block), bf16),
     ]
     sems_b = [
         dma((2,)),
@@ -1162,6 +1276,10 @@
         dma((2, chunks)),
         dma((2, count_s)),
         dma((slots,)),
+        dma((count_t,)),
+        dma((count_t,)),
+        dma((2, count_s)),
+        dma((slots // count_t, count_t)),
     ]
     specs = [vmem] * len(args)
     for place in (2, 6, 7, 9, 12, 13, 16):
@@ -1252,7 +1370,7 @@
         down_scale,
     )
     if fast_layer(args):
-        return layer(args, (4, 6, 4, 4))
+        return layer(args, (4, 8, 4))
     tp_count = lax.axis_size("tp")
     tp_index = lax.axis_index("tp")
     share_cols = D // tp_count

time: 111 us -> 107 us (0.964); the launches traced: 110 us -> 104 us
  Pallas kernels: 109 us -> 104 us
    pallas_call x1, Pallas kernels: 109 us -> 104 us  [layer(): pl.pallas_call(functools.partial(layer_kernel, lags, counts), out_shape=p...]
where the time goes in v5:
time: 107 us; the launch traced here: 104 us
  Pallas kernels  104 us (97%)
    pallas_call x1, Pallas kernels, layer(): pl.pallas_call(functools.partial(layer_kernel, lags, counts), out_shape=p...  104 us

profile of v5, /device:TPU:0, one launch (start us, length us, event | category | flops | bytes accessed | tf_op | source)
XLA Modules:
  0.0 104.4 jit_solution(11741374959867150022)
XLA Ops:
  0.0 103.7 %layer.1 = f32[64,1280]{1,0:T(8,128)S(1)} custom-call(bf16[64,5120]{1,0:T(8,128)(2,1)} %refs_0_.1, f32[5120]{0:T(1024)} %refs_1_.1, s32[1280,1280]{1,0:T(8,128)} %refs_2_.1, f32[1280]{0:T(1024)} %refs_3_.1, f32[128]{0:T(128)} %refs_4_.1, f32[128]{0:T(128)} %refs_5_.1, bf16[1,16,128,512]{3,2,1,0:T(8,128)(2,1)} %refs_6_.1, bf16[1,16,128,512]{3,2,1,0:T(8,128)(2,1)} %refs_7_.1, ...), custom_call_target="tpu_custom_call" | custom-call | tf_op jit(solution)/shard_map/layer/pallas_call | solution.py:1296
  103.8 0.7 convert_element_type.3

commit v6 on v4

--- a/solution.py
+++ b/solution.py
@@ -717,9 +717,20 @@
 def mlp_phase(here, lags, scales, mlp_buffers, scratch, sems, attention, out_ref):
     g, t, s, count_g, count_t, count_s = here
     gate_scale, up_scale, down_scale, order_ref = scales
-    lag, back_lag, far_lag, back_start = lags
+    lag, back_lag, far_lag, second_lag = lags
     gate_v, up_v, down_v, x_v, mid_v = mlp_buffers
-    partial, sum_recv, act, total, part_send, part_recv = scratch
+    (
+        partial,
+        sum_recv,
+        act,
+        total,
+        part_send,
+        part_recv,
+        stage_send,
+        stage_recv,
+        last_send,
+        last_recv,
+    ) = scratch
     (
         sum_send_sem,
         sum_recv_sem,
@@ -727,6 +738,10 @@
         act_recv_sem,
         part_send_sem,
         part_recv_sem,
+        stage_send_sem,
+        stage_recv_sem,
+        last_send_sem,
+        last_recv_sem,
     ) = sems
     swaps, loads, mid_wait, x_wait, finish = attention
     rows = x_v.shape[0]
@@ -846,14 +861,30 @@
 
         return carry
 
+    def down_step(sides, j):
+        slab = LANES // 4
+        words = pl.ds(pl.multiple_of(j * slab, slab), slab)
+        weights = jnp.concatenate(
+            [unpack_slab(down_v[index, words, :]) for index in range(2)], axis=1
+        )
+        for side in sides:
+            total[(1 - side) * half : (2 - side) * half] += jnp.dot(
+                act[side, j], weights, preferred_element_type=jnp.float32
+            )
+
     def end_loop(j, carry):
         for side in range(2):
 
             @pl.when(depth_of(side) == last)
             def _():
                 end_step(side, j)
+                down_step((side,), j)
 
         return carry
+
+    near_depth = jnp.minimum(s, last - s)
+    far_depth = jnp.maximum(s, last - s)
+    second = jnp.where(is_end, last * back_lag + second_lag, chunks + far_depth * back_lag)
 
     def back_step(i, carry):
         for side in range(2):
@@ -863,27 +894,100 @@
             @pl.when((depth > 0) & (j >= 0) & (j < chunks))
             def _():
                 act_step(side, j)
-
-        j = i - jnp.maximum(s, last - s) * back_lag
-
-        @pl.when((j >= 0) & (j < chunks))
+                down_step((side,), j)
+
+        @pl.when(jnp.logical_not(is_end) & (i == chunks + near_depth * back_lag))
         def _():
-            @pl.when(j == 0)
-            def _():
-                loads[2].wait()
-                swaps[2].wait_recv()
-
-            slab = LANES // 4
-            words = pl.ds(pl.multiple_of(j * slab, slab), slab)
-            weights = jnp.concatenate(
-                [unpack_slab(down_v[index, words, :]) for index in range(2)], axis=1
-            )
-            for side in range(2):
-                total[(1 - side) * half : (2 - side) * half] += jnp.dot(
-                    act[side, j], weights, preferred_element_type=jnp.float32
+            stage_rows()
+
+        @pl.when(i == second)
+        def _():
+            pass_rows()
+
+        return carry
+
+    per_share = count_g * count_s // count_t
+
+    groups = count_s // 2
+    quarter = group_rows // count_t
+    low_half = s < groups
+    near_base = jnp.where(low_half, 0, groups)
+    cross_base = groups - near_base
+
+    def target_of(index):
+        number = jnp.where(index == 0, g, count_g - 1 - g) * count_s + s
+        return number // per_share, lax.rem(number, per_share)
+
+    def part_copy(index, k, ss):
+        owner, place = target_of(index)
+        slot = t * per_share + place
+        return owner, slot, pltpu.make_async_remote_copy(
+            src_ref=part_send.at[index, k],
+            dst_ref=part_recv.at[slot],
+            send_sem=part_send_sem.at[index, k],
+            recv_sem=part_recv_sem.at[slot],
+            device_id={"tp": owner, "src": ss},
+            device_id_type=MESH,
+        )
+
+    def stage_copy(peer):
+        return pltpu.make_async_remote_copy(
+            src_ref=stage_send.at[peer],
+            dst_ref=stage_recv.at[t],
+            send_sem=stage_send_sem.at[peer],
+            recv_sem=stage_recv_sem.at[t],
+            device_id={"tp": peer},
+            device_id_type=MESH,
+        )
+
+    def stage_arrival(peer):
+        return pltpu.make_async_remote_copy(
+            src_ref=stage_send.at[peer],
+            dst_ref=stage_recv.at[peer],
+            send_sem=stage_send_sem.at[peer],
+            recv_sem=stage_recv_sem.at[peer],
+            device_id={"tp": peer},
+            device_id_type=MESH,
+        )
+
+    def last_copy(index, k, place, slot, owner):
+        return pltpu.make_async_remote_copy(
+            src_ref=last_send.at[index, k],
+            dst_ref=last_recv.at[place, slot],
+            send_sem=last_send_sem.at[index, k],
+            recv_sem=last_recv_sem.at[place, slot],
+            device_id={"tp": owner, "src": cross_base + k},
+            device_id_type=MESH,
+        )
+
+    def quarter_rows(k, tt):
+        start = (cross_base + k) * group_rows + tt * quarter
+        return pl.ds(pl.multiple_of(start, quarter), quarter)
+
+    def stage_rows():
+        for shift in range(1, count_t):
+            peer = lax.rem(t + shift, count_t)
+            for k in range(groups):
+                stage_send[peer, k] = total[quarter_rows(k, peer), :].astype(jnp.bfloat16)
+            stage_copy(peer).start()
+
+    def pass_rows():
+        for shift in range(1, count_t):
+            stage_arrival(lax.rem(t + shift, count_t)).wait_recv()
+        for k in range(groups):
+            value = total[quarter_rows(k, t), :]
+            for turn in range(1, count_t):
+                value += stage_recv[lax.rem(t + turn, count_t), k].astype(jnp.float32)
+            for index in range(2):
+                owner, place = target_of(index)
+                last_send[index, k] = value[:, index * block : (index + 1) * block].astype(
+                    jnp.bfloat16
                 )
-
-        return carry
+                last_copy(index, k, place, t, owner).start()
+
+    def near_rows(k):
+        ss = near_base + lax.rem(s - near_base + 1 + k, groups)
+        return ss, pl.ds(pl.multiple_of(ss * group_rows, group_rows), group_rows)
 
     for index in range(2):
         loads[index].wait()
@@ -891,31 +995,36 @@
     with jax.named_scope("mlp_loop"):
         lax.fori_loop(0, chunks + far, step, 0)
     with jax.named_scope("end_loop"):
+        loads[2].wait()
+        swaps[2].wait_recv()
         lax.fori_loop(0, chunks, end_loop, 0)
+
+        @pl.when(is_end)
+        def _():
+            stage_rows()
+
     with jax.named_scope("back_loop"):
         lax.fori_loop(0, chunks + last * back_lag, back_step, 0)
 
-    per_share = count_g * count_s // count_t
-
-    def part_copy(index, ss):
-        number = jnp.where(index == 0, g, count_g - 1 - g) * count_s + s
-        owner = number // per_share
-        slot = t * per_share + lax.rem(number, per_share)
-        return owner, slot, pltpu.make_async_remote_copy(
-            src_ref=part_send.at[index, ss],
-            dst_ref=part_recv.at[slot],
-            send_sem=part_send_sem.at[index, ss],
-            recv_sem=part_recv_sem.at[slot],
-            device_id={"tp": owner, "src": ss},
-            device_id_type=MESH,
-        )
+    def drain():
+        with jax.named_scope("drain"):
+            finish()
+            for side in range(2):
+                depth = depth_of(side)
+
+                @pl.when(depth < last)
+                def _():
+                    whole_copy(partial, side, sum_send_sem).wait_send()
+
+                @pl.when(depth > 0)
+                def _():
+                    whole_copy(act, side, act_send_sem).wait_send()
 
     with jax.named_scope("part_send"):
-        for shift in range(count_s):
-            ss = send_order(s, count_s, shift)
-            row = pl.ds(pl.multiple_of(ss * group_rows, group_rows), group_rows)
+        for k in range(groups):
+            ss, row = near_rows(k)
             for index in range(2):
-                owner, slot, copy = part_copy(index, ss)
+                owner, slot, copy = part_copy(index, k, ss)
                 piece = total[row, index * block : (index + 1) * block].astype(jnp.bfloat16)
                 mine = (owner == t) & (ss == s)
 
@@ -925,66 +1034,60 @@
 
                 @pl.when(jnp.logical_not(mine))
                 def _():
-                    part_send[index, ss] = piece
+                    part_send[index, k] = piece
                     copy.start()
 
-    with jax.named_scope("drain"):
-        finish()
-        for side in range(2):
-            depth = depth_of(side)
-
-            @pl.when(depth < last)
-            def _():
-                whole_copy(partial, side, sum_send_sem).wait_send()
-
-            @pl.when(depth > 0)
-            def _():
-                whole_copy(act, side, act_send_sem).wait_send()
-
+    drain()
+    mid_wait()
     with jax.named_scope("part_wait"):
-        for slot in range(count_t * per_share):
-            number = t * per_share + slot % per_share
-            from_me = (slot // per_share == t) & (lax.rem(number, count_s) == s)
-
-            @pl.when(jnp.logical_not(from_me))
-            def _():
-                pltpu.make_async_remote_copy(
-                    src_ref=part_send.at[0, 0],
-                    dst_ref=part_recv.at[slot],
-                    send_sem=part_send_sem.at[0, 0],
-                    recv_sem=part_recv_sem.at[slot],
-                    device_id={"tp": t, "src": s},
-                    device_id_type=MESH,
-                ).wait_recv()
-
-    mid_wait()
-    with jax.named_scope("part_sum"):
         for place in range(per_share):
-            value = part_recv[place].astype(jnp.float32)
-            for tt in range(1, count_t):
-                value += part_recv[tt * per_share + place].astype(jnp.float32)
+            origin = lax.rem(t * per_share + place, count_s)
+            crosses = (origin < groups) != low_half
             columns = slice(place * block, (place + 1) * block)
             scale_at = pl.ds(pl.multiple_of((t * per_share + place) * block, LANES), block)
-            out_ref[:, columns] = (
-                mid_v[:, columns].astype(jnp.float32) + value * down_scale[scale_at].reshape(1, block)
-            )
-
-    for ss in range(count_s):
+
+            @pl.when(jnp.logical_not(crosses))
+            def _():
+                for tt in range(count_t):
+
+                    @pl.when((tt != t) | (origin != s))
+                    def _():
+                        pltpu.make_async_remote_copy(
+                            src_ref=part_send.at[0, 0],
+                            dst_ref=part_recv.at[tt * per_share + place],
+                            send_sem=part_send_sem.at[0, 0],
+                            recv_sem=part_recv_sem.at[tt * per_share + place],
+                            device_id={"tp": tt},
+                            device_id_type=MESH,
+                        ).wait_recv()
+
+                value = part_recv[place].astype(jnp.float32)
+                for tt in range(1, count_t):
+                    value += part_recv[tt * per_share + place].astype(jnp.float32)
+                out_ref[:, columns] = mid_v[:, columns].astype(jnp.float32) + value * down_scale[
+                    scale_at
+                ].reshape(1, block)
+
+            @pl.when(crosses)
+            def _():
+                for tt in range(count_t):
+                    last_copy(0, 0, place, tt, t).wait_recv()
+                    row = slice(tt * quarter, (tt + 1) * quarter)
+                    out_ref[row, columns] = mid_v[row, columns].astype(jnp.float32) + last_recv[
+                        place, tt
+                    ].astype(jnp.float32) * down_scale[scale_at].reshape(1, block)
+
+    for shift in range(1, count_t):
+        stage_copy(lax.rem(t + shift, count_t)).wait_send()
+    for k in range(groups):
+        ss, row = near_rows(k)
         for index in range(2):
-            owner, slot, copy = part_copy(index, ss)
+            owner, place = target_of(index)
+            last_copy(index, k, place, t, owner).wait_send()
 
             @pl.when((owner != t) | (ss != s))
             def _():
-                copy.wait_send()
-
-
-def send_order(s, count_s, shift):
-    if count_s % 2:
-        return lax.rem(s + 1 + shift, count_s)
-    size = count_s // 2
-    other = jnp.where(s < size, size, 0)
-    base = other if shift < size else size - other
-    return base + lax.rem(s + 1 + shift, size)
+                part_copy(index, k, ss)[2].wait_send()
 
 
 def layer_kernel(lags, counts, *refs):
@@ -1090,7 +1193,7 @@
     share = model // count_t
     slots = count_g * count_s
     steps = 10 if w_qkv.shape[0] % 320 == 0 else w_qkv.shape[0] // 32
-    out_steps = 10 if model % (10 * LANES) == 0 else model // LANES
+    out_steps = 5 if model % (5 * LANES) == 0 else model // LANES
     qkv_columns = w_qkv.shape[1]
     head_rows = QUERY_HEADS * mine
     bf16, f32, i32 = jnp.bfloat16, jnp.float32, jnp.int32
@@ -1152,16 +1255,24 @@
         pltpu.VMEM((2, chunks, half, 2 * LANES), bf16),
         pltpu.VMEM((2, chunks, half, LANES), bf16),
         pltpu.VMEM((rows, depth), f32),
-        pltpu.VMEM((2, count_s, group_rows, block), bf16),
+        pltpu.VMEM((2, count_s // 2, group_rows, block), bf16),
         pltpu.VMEM((slots, group_rows, block), bf16),
+        pltpu.VMEM((count_t, count_s // 2, mine, depth), bf16),
+        pltpu.VMEM((count_t, count_s // 2, mine, depth), bf16),
+        pltpu.VMEM((2, count_s // 2, mine, block), bf16),
+        pltpu.VMEM((slots // count_t, count_t, mine, block), bf16),
     ]
     sems_b = [
         dma((2,)),
         dma((2, chunks)),
         dma((2,)),
         dma((2, chunks)),
-        dma((2, count_s)),
+        dma((2, count_s // 2)),
         dma((slots,)),
+        dma((count_t,)),
+        dma((count_t,)),
+        dma((2, count_s // 2)),
+        dma((slots // count_t, count_t)),
     ]
     specs = [vmem] * len(args)
     for place in (2, 6, 7, 9, 12, 13, 16):
@@ -1194,7 +1305,7 @@
     rows, model = hidden_in.shape
     return (
         grp == 2
-        and src > 1
+        and src % 2 == 0
         and tp > 1
         and (grp * src) % tp == 0
         and rows % (16 * tp) == 0
@@ -1252,7 +1363,7 @@
         down_scale,
     )
     if fast_layer(args):
-        return layer(args, (4, 6, 4, 4))
+        return layer(args, (4, 8, 4, 14))
     tp_count = lax.axis_size("tp")
     tp_index = lax.axis_index("tp")
     share_cols = D // tp_count

time: 111 us -> 105 us (0.946)
  Pallas kernels: 109 us -> 104 us
    pallas_call x1, Pallas kernels: 109 us -> 104 us  [layer(): pl.pallas_call(functools.partial(layer_kernel, lags, counts), out_shape=p...]
where the time goes in v6:
time: 105 us
  Pallas kernels  104 us (99%)
    pallas_call x1, Pallas kernels, layer(): pl.pallas_call(functools.partial(layer_kernel, lags, counts), out_shape=p...  104 us

profile of v6, /device:TPU:0, one launch (start us, length us, event | category | flops | bytes accessed | tf_op | source)
XLA Modules:
  0.0 104.6 jit_solution(13658972048255606408)
XLA Ops:
  0.0 103.9 %layer.1 = f32[64,1280]{1,0:T(8,128)S(1)} custom-call(bf16[64,5120]{1,0:T(8,128)(2,1)} %refs_0_.1, f32[5120]{0:T(1024)} %refs_1_.1, s32[1280,1280]{1,0:T(8,128)} %refs_2_.1, f32[1280]{0:T(1024)} %refs_3_.1, f32[128]{0:T(128)} %refs_4_.1, f32[128]{0:T(128)} %refs_5_.1, bf16[1,16,128,512]{3,2,1,0:T(8,128)(2,1)} %refs_6_.1, bf16[1,16,128,512]{3,2,1,0:T(8,128)(2,1)} %refs_7_.1, ...), custom_call_target="tpu_custom_call" | custom-call | tf_op jit(solution)/shard_map/layer/pallas_call | solution.py:1289
  103.9 0.7 convert_element_type.3

commit v7 on v6

--- a/solution.py
+++ b/solution.py
@@ -735,7 +735,6 @@
         sum_send_sem,
         sum_recv_sem,
         act_send_sem,
-        act_recv_sem,
         part_send_sem,
         part_recv_sem,
         stage_send_sem,
@@ -773,7 +772,7 @@
             src_ref=act.at[side, j],
             dst_ref=act.at[side, j],
             send_sem=act_send_sem.at[side],
-            recv_sem=act_recv_sem.at[side, j],
+            recv_sem=sum_recv_sem.at[side, j],
             device_id={"src": toward(1 - side)},
             device_id_type=MESH,
         )
@@ -1193,7 +1192,7 @@
     share = model // count_t
     slots = count_g * count_s
     steps = 10 if w_qkv.shape[0] % 320 == 0 else w_qkv.shape[0] // 32
-    out_steps = 5 if model % (5 * LANES) == 0 else model // LANES
+    out_steps = 8 if model % (8 * LANES) == 0 else model // LANES
     qkv_columns = w_qkv.shape[1]
     head_rows = QUERY_HEADS * mine
     bf16, f32, i32 = jnp.bfloat16, jnp.float32, jnp.int32
@@ -1266,7 +1265,6 @@
         dma((2,)),
         dma((2, chunks)),
         dma((2,)),
-        dma((2, chunks)),
         dma((2, count_s // 2)),
         dma((slots,)),
         dma((count_t,)),

time: 105 us -> 104 us (level)
  no operation moved by 1% of the time
where the time goes in v7:
time: 104 us
  Pallas kernels  103 us (99%)
    pallas_call x1, Pallas kernels, layer(): pl.pallas_call(functools.partial(layer_kernel, lags, counts), out_shape=p...  103 us

profile of v7, /device:TPU:0, one launch (start us, length us, event | category | flops | bytes accessed | tf_op | source)
XLA Modules:
  0.0 104.1 jit_solution(14865125581517057603)
XLA Ops:
  0.0 103.4 %layer.1 = f32[64,1280]{1,0:T(8,128)S(1)} custom-call(bf16[64,5120]{1,0:T(8,128)(2,1)} %refs_0_.1, f32[5120]{0:T(1024)} %refs_1_.1, s32[1280,1280]{1,0:T(8,128)} %refs_2_.1, f32[1280]{0:T(1024)} %refs_3_.1, f32[128]{0:T(128)} %refs_4_.1, f32[128]{0:T(128)} %refs_5_.1, bf16[1,16,128,512]{3,2,1,0:T(8,128)(2,1)} %refs_6_.1, bf16[1,16,128,512]{3,2,1,0:T(8,128)(2,1)} %refs_7_.1, ...), custom_call_target="tpu_custom_call" | custom-call | tf_op jit(solution)/shard_map/layer/pallas_call | solution.py:1287
  103.4 0.7 convert_element_type.3
